TPU v7x, 256 devices: a whole 4x4x8 slice. The times are simulated.
256 devices in a mesh: gz: 256 (over z, y, x, core).
Axes of the slice: x: 4, y: 4, z: 8, core: 2. Of those that a mesh axis runs over, the one named last changes fastest.
Arguments:
- coefficient: float32 [512, 512, 512], P('gz'), may hold values from 0.2 to 1.3
- initial_field: float32 [512, 512, 512], P('gz'), may hold values from -6 to 6
- observed: float32 [512, 512, 512], P('gz'), may hold values from -6 to 6
- misfit_weight: float32 [512, 512, 512], P('gz'), may hold values from 0.5 to 6, as said below
Outputs:
- coeff_gradient: float32 [512, 512, 512], P('gz')
- adjoint_field: float32 [512, 512, 512], P('gz')
- misfit: float32 [], replicated
Inputs may be any that keep to these rules, and one draw needn't show every extreme that they name: `misfit_weight`: positive cell weights.
All inputs are finite; a program needn't handle non-finite values.
Results may differ from a plain program's by a relative error of at most 0.00002.
Values sent between devices are 32-bit elements; how exact they have to be, the bound alone decides.
A program may use at most 128 MiB of HBM per device.

v0:
```python
import functools

import jax
import jax.numpy as jnp
from jax import lax
from jax.sharding import Mesh
from jax.sharding import PartitionSpec as P

ITERS = 4
GZ = ("gz_0", "gz_1", "gz_2", "gz_3")


time_step = 0.125


def extended(shard, sides, width):
    for axis, dim in sides:
        count, length = (lax.axis_size(axis), shard.shape[dim])
        up = [(i, (i + 1) % count) for i in range(count - 1)]
        down = [(j, i) for i, j in up]
        last = lax.slice_in_dim(shard, length - width, length, axis=dim)
        initial = lax.slice_in_dim(shard, 0, width, axis=dim)
        before = lax.ppermute(last, axis, up)
        after = lax.ppermute(initial, axis, down)
        shard = jnp.concatenate([before, shard, after], axis=dim)
    return shard


def by_axis(shard, axes):
    return functools.reduce(lax.psum, axes, shard)


def lateral(field):
    padded = jnp.pad(field, ((0, 0), (1, 1), (1, 1)))
    beside = padded[:, 2:, 1:-1] + padded[:, :-2, 1:-1]
    return beside + padded[:, 1:-1, 2:] + padded[:, 1:-1, :-2]


def forward_slope(state):
    padded = extended(state, ((GZ, 0),), 1)
    return lateral(state) + padded[2:] + padded[:-2] - 6.0 * state


def adjoint_slope(moved):
    padded = extended(moved, ((GZ, 0),), 1)
    upper = padded[2:]
    lower = padded[:-2]
    return lateral(moved) + upper + lower - 6.0 * moved


def on_device(coefficient, initial_field, observed, misfit_weight):
    slopes = []
    state = initial_field
    for step in range(ITERS):
        slope = forward_slope(state)
        slopes.append(slope)
        state = state + time_step * coefficient * slope
    resid = state - observed
    weighted = misfit_weight * resid
    total = by_axis(jnp.sum(weighted * resid), GZ)
    cells = lax.axis_size(GZ) * coefficient.shape[0] * coefficient.shape[1] * coefficient.shape[2]
    misfit = jnp.sqrt(total / cells + 1e-06)
    gradient = jnp.zeros_like(coefficient)
    adjoint = weighted
    for step in reversed(range(ITERS)):
        gradient = gradient + time_step * adjoint * slopes[step]
        adjoint = adjoint + time_step * adjoint_slope(coefficient * adjoint)
    gradient = gradient / misfit
    adjoint = adjoint / misfit
    return (gradient, adjoint, misfit)


def solution(mesh):
    torus = Mesh(mesh.devices.reshape(8, 4, 4, 2), ("gz_0", "gz_1", "gz_2", "gz_3"))
    return jax.shard_map(
        on_device,
        mesh=torus,
        in_specs=(P(GZ, None, None), P(GZ, None, None), P(GZ, None, None), P(GZ, None, None)),
        out_specs=(P(GZ, None, None), P(GZ, None, None), P()),
        check_vma=False,
    )
```

profile of v0, /device:TPU:127, one launch (start us, length us, event | category | flops | bytes accessed | tf_op | source)
XLA Modules:
  0.0 258.0 jit_solution(2643937728559244340)
XLA Ops:
  5.1 8.4 %collective-permute-start.1 = (f32[1,512,512]{2,1,0:T(8,128)S(1)}, f32[1,512,512]{2,1,0:T(8,128)S(1)}, u32[]{:S(2)}, u32[]{:S(2)}) collective-permute-start(f32[1,512,512]{2,1,0:T(8,128)S(1)} %get-tuple-element.36), channel_id=1, source_target_pairs={{0,1},{1,2},{2,3},{3,4},{4,5},{5,6},{6,7},{7,8},{8,9},{9,10},{10,1... | collective-permute-start | bytes 3145736 | tf_op jit(solution)/shard_map/ppermute | solution.py:23
  13.5 10.5 %collective-permute-done = f32[1,512,512]{2,1,0:T(8,128)S(1)} collective-permute-done((f32[1,512,512]{2,1,0:T(8,128)S(1)}, f32[1,512,512]{2,1,0:T(8,128)S(1)}, u32[]{:S(2)}, u32[]{:S(2)}) %collective-permute-start) | collective-permute-done | bytes 1048608 | tf_op jit(solution)/shard_map/ppermute | solution.py:24
  25.3 3.2 %multiply_add_fusion.2 = (f32[2,512,512]{2,1,0:T(8,128)S(1)}, f32[2,512,512]{2,1,0:T(8,128)}) fusion(f32[2,512,512]{2,1,0:T(8,128)S(1)} %copy-done.4, f32[2,512,512]{2,1,0:T(8,128)S(1)} %copy-done, f32[1,512,512]{2,1,0:T(8,128)S(1)} %collective-permute-done.1, f32[1,512,512]{2,1,0:T(8,128)S(1)} %collective-permute-done), kind=kLoop, calls=%fused_computation.110 | loop fusion | flops 6291456 | bytes 10485760 | tf_op jit(solution)/shard_map/add | solution.py:57
  30.5 9.8 %collective-permute-start.3 = (f32[1,512,512]{2,1,0:T(8,128)S(1)}, f32[1,512,512]{2,1,0:T(8,128)S(1)}, u32[]{:S(2)}, u32[]{:S(2)}) collective-permute-start(f32[1,512,512]{2,1,0:T(8,128)S(1)} %get-tuple-element.34), channel_id=1, source_target_pairs={{0,1},{1,2},{2,3},{3,4},{4,5},{5,6},{6,7},{7,8},{8,9},{9,10},{10,1... | collective-permute-start | bytes 3145736 | tf_op jit(solution)/shard_map/ppermute | solution.py:23
  40.4 10.5 %collective-permute-done.2 = f32[1,512,512]{2,1,0:T(8,128)S(1)} collective-permute-done((f32[1,512,512]{2,1,0:T(8,128)S(1)}, f32[1,512,512]{2,1,0:T(8,128)S(1)}, u32[]{:S(2)}, u32[]{:S(2)}) %collective-permute-start.2) | collective-permute-done | bytes 1048608 | tf_op jit(solution)/shard_map/ppermute | solution.py:24
  57.4 9.8 %collective-permute-start.5 = (f32[1,512,512]{2,1,0:T(8,128)S(1)}, f32[1,512,512]{2,1,0:T(8,128)S(1)}, u32[]{:S(2)}, u32[]{:S(2)}) collective-permute-start(f32[1,512,512]{2,1,0:T(8,128)S(1)} %get-tuple-element.32), channel_id=1, source_target_pairs={{0,1},{1,2},{2,3},{3,4},{4,5},{5,6},{6,7},{7,8},{8,9},{9,10},{10,1... | collective-permute-start | bytes 3145736 | tf_op jit(solution)/shard_map/ppermute | solution.py:23
  67.2 10.5 %collective-permute-done.4 = f32[1,512,512]{2,1,0:T(8,128)S(1)} collective-permute-done((f32[1,512,512]{2,1,0:T(8,128)S(1)}, f32[1,512,512]{2,1,0:T(8,128)S(1)}, u32[]{:S(2)}, u32[]{:S(2)}) %collective-permute-start.4) | collective-permute-done | bytes 1048608 | tf_op jit(solution)/shard_map/ppermute | solution.py:24
  78.9 3.2 %multiply_add_fusion = (f32[2,512,512]{2,1,0:T(8,128)S(1)}, f32[2,512,512]{2,1,0:T(8,128)}) fusion(f32[2,512,512]{2,1,0:T(8,128)S(1)} %get-tuple-element.15, f32[2,512,512]{2,1,0:T(8,128)S(1)} %copy-done, f32[1,512,512]{2,1,0:T(8,128)S(1)} %collective-permute-done.5, f32[1,512,512]{2,1,0:T(8,128)S(1)} %collective-permute-done.4), kind=kLoop, calls=%fused_computation.108 | loop fusion | flops 6291456 | bytes 10485760 | tf_op jit(solution)/shard_map/add | solution.py:57
  84.4 9.9 %collective-permute-start.7 = (f32[1,512,512]{2,1,0:T(8,128)S(1)}, f32[1,512,512]{2,1,0:T(8,128)S(1)}, u32[]{:S(2)}, u32[]{:S(2)}) collective-permute-start(f32[1,512,512]{2,1,0:T(8,128)S(1)} %get-tuple-element.30), channel_id=1, source_target_pairs={{0,1},{1,2},{2,3},{3,4},{4,5},{5,6},{6,7},{7,8},{8,9},{9,10},{10,1... | collective-permute-start | bytes 3145736 | tf_op jit(solution)/shard_map/ppermute | solution.py:23
  94.3 10.4 %collective-permute-done.6 = f32[1,512,512]{2,1,0:T(8,128)S(1)} collective-permute-done((f32[1,512,512]{2,1,0:T(8,128)S(1)}, f32[1,512,512]{2,1,0:T(8,128)S(1)}, u32[]{:S(2)}, u32[]{:S(2)}) %collective-permute-start.6) | collective-permute-done | bytes 1048608 | tf_op jit(solution)/shard_map/ppermute | solution.py:24
  106.1 3.5 %add_subtract_fusion = (f32[2,512,512]{2,1,0:T(8,128)S(1)}, f32[2,512,512]{2,1,0:T(8,128)}) fusion(f32[2,512,512]{2,1,0:T(8,128)S(1)} %copy-done.6, f32[2,512,512]{2,1,0:T(8,128)S(1)} %get-tuple-element.13, f32[2,512,512]{2,1,0:T(8,128)S(1)} %copy-done, f32[1,512,512]{2,1,0:T(8,128)S(1)} %collective-permute-done.7, f32[1,512,512]{2,1,0:T(8,128)S(1)} %collective-permute-done.6), kind=kLoop, calls=%fused_computation.107 | loop fusion | flops 6815744 | bytes 12582912 | tf_op jit(solution)/shard_map/sub | solution.py:58
  113.4 9.8 %collective-permute-start.9 = (f32[1,512,512]{2,1,0:T(8,128)S(1)}, f32[1,512,512]{2,1,0:T(8,128)S(1)}, u32[]{:S(2)}, u32[]{:S(2)}) collective-permute-start(f32[1,512,512]{2,1,0:T(8,128)S(1)} %get-tuple-element.28), channel_id=1, source_target_pairs={{0,1},{1,2},{2,3},{3,4},{4,5},{5,6},{6,7},{7,8},{8,9},{9,10},{10,1... | collective-permute-start | bytes 3145736 | tf_op jit(solution)/shard_map/ppermute | solution.py:23
  123.2 10.5 %collective-permute-done.8 = f32[1,512,512]{2,1,0:T(8,128)S(1)} collective-permute-done((f32[1,512,512]{2,1,0:T(8,128)S(1)}, f32[1,512,512]{2,1,0:T(8,128)S(1)}, u32[]{:S(2)}, u32[]{:S(2)}) %collective-permute-start.8) | collective-permute-done | bytes 1048608 | tf_op jit(solution)/shard_map/ppermute | solution.py:24
  139.5 9.8 %collective-permute-start.11 = (f32[1,512,512]{2,1,0:T(8,128)S(1)}, f32[1,512,512]{2,1,0:T(8,128)S(1)}, u32[]{:S(2)}, u32[]{:S(2)}) collective-permute-start(f32[1,512,512]{2,1,0:T(8,128)S(1)} %get-tuple-element.26), channel_id=1, source_target_pairs={{0,1},{1,2},{2,3},{3,4},{4,5},{5,6},{6,7},{7,8},{8,9},{9,10},{10,1... | collective-permute-start | bytes 3145736 | tf_op jit(solution)/shard_map/ppermute | solution.py:23
  149.3 10.5 %collective-permute-done.10 = f32[1,512,512]{2,1,0:T(8,128)S(1)} collective-permute-done((f32[1,512,512]{2,1,0:T(8,128)S(1)}, f32[1,512,512]{2,1,0:T(8,128)S(1)}, u32[]{:S(2)}, u32[]{:S(2)}) %collective-permute-start.10) | collective-permute-done | bytes 1048608 | tf_op jit(solution)/shard_map/ppermute | solution.py:24
  165.5 10.0 %collective-permute-start.13 = (f32[1,512,512]{2,1,0:T(8,128)S(1)}, f32[1,512,512]{2,1,0:T(8,128)S(1)}, u32[]{:S(2)}, u32[]{:S(2)}) collective-permute-start(f32[1,512,512]{2,1,0:T(8,128)S(1)} %get-tuple-element.24), channel_id=1, source_target_pairs={{0,1},{1,2},{2,3},{3,4},{4,5},{5,6},{6,7},{7,8},{8,9},{9,10},{10,1... | collective-permute-start | bytes 3145736 | tf_op jit(solution)/shard_map/ppermute | solution.py:23
  175.5 10.4 %collective-permute-done.12 = f32[1,512,512]{2,1,0:T(8,128)S(1)} collective-permute-done((f32[1,512,512]{2,1,0:T(8,128)S(1)}, f32[1,512,512]{2,1,0:T(8,128)S(1)}, u32[]{:S(2)}, u32[]{:S(2)}) %collective-permute-start.12) | collective-permute-done | bytes 1048608 | tf_op jit(solution)/shard_map/ppermute | solution.py:24
  187.1 3.4 %fusion.57 = (f32[2,512,512]{2,1,0:T(8,128)S(1)}, f32[2,512,512]{2,1,0:T(8,128)}) fusion(f32[2,512,512]{2,1,0:T(8,128)S(1)} %copy-done, f32[2,512,512]{2,1,0:T(8,128)S(1)} %get-tuple-element.8, f32[2,512,512]{2,1,0:T(8,128)S(1)} %get-tuple-element.7, f32[1,512,512]{2,1,0:T(8,128)S(1)} %collective-permute-done.13, f32[1,512,512]{2,1,0:T(8,128)S(1)} %collective-permute-done.12), kind=kLoop, calls=%fused_computation.111 | loop fusion | flops 6291456 | bytes 12582912 | tf_op jit(solution)/shard_map/mul | solution.py:67
  195.3 9.8 %collective-permute-start.15 = (f32[1,512,512]{2,1,0:T(8,128)}, f32[1,512,512]{2,1,0:T(8,128)}, u32[]{:S(2)}, u32[]{:S(2)}) collective-permute-start(f32[1,512,512]{2,1,0:T(8,128)} %get-tuple-element.22), channel_id=1, source_target_pairs={{0,1},{1,2},{2,3},{3,4},{4,5},{5,6},{6,7},{7,8},{8,9},{9,10},{10,1... | collective-permute-start | bytes 3145736 | tf_op jit(solution)/shard_map/ppermute | solution.py:23
  205.1 20.4 %psum.28 = f32[]{:T(128)} all-reduce(f32[]{:T(128)} %get-tuple-element.5), channel_id=1, replica_groups=mesh['gz_0'=8,'gz_1'=4,'gz_2'=4,'gz_3'=2] {'gz_0'}, use_global_device_ids=true, to_apply=%region_1.2 | all-reduce | flops 1 | bytes 8 | tf_op jit(solution)/shard_map/psum | solution.py:30
  225.5 6.4 %psum.29 = f32[]{:T(128)} all-reduce(f32[]{:T(128)} %psum.28), channel_id=1, replica_groups=mesh['gz_0'=8,'gz_1'=4,'gz_2'=4,'gz_3'=2] {'gz_1'}, use_global_device_ids=true, to_apply=%region_2.3 | all-reduce | flops 1 | bytes 8 | tf_op jit(solution)/shard_map/psum | solution.py:30
  231.8 6.4 %psum.30 = f32[]{:T(128)} all-reduce(f32[]{:T(128)} %psum.29), channel_id=1, replica_groups=mesh['gz_0'=8,'gz_1'=4,'gz_2'=4,'gz_3'=2] {'gz_2'}, use_global_device_ids=true, to_apply=%region_3.4 | all-reduce | flops 1 | bytes 8 | tf_op jit(solution)/shard_map/psum | solution.py:30
  238.2 4.9 %psum.31 = f32[]{:T(128)} all-reduce(f32[]{:T(128)} %psum.30), channel_id=1, replica_groups=mesh['gz_0'=8,'gz_1'=4,'gz_2'=4,'gz_3'=2] {'gz_3'}, use_global_device_ids=true, to_apply=%region_4.5 | all-reduce | flops 1 | bytes 8 | tf_op jit(solution)/shard_map/psum | solution.py:30
  243.8 13.0 %fusion.56 = (f32[2,512,512]{2,1,0:T(8,128)}, f32[2,512,512]{2,1,0:T(8,128)}) fusion(f32[2,512,512]{2,1,0:T(8,128)} %get-tuple-element.4, f32[2,512,512]{2,1,0:T(8,128)} %copy-done.1, f32[1,512,512]{2,1,0:T(8,128)} %collective-permute-done.15, f32[1,512,512]{2,1,0:T(8,128)S(1)} %collective-permute-done.14, f32[]{:T(128)} %sqrt.3, ...), kind=kLoop, calls=%fused_computation.88 | loop fusion | flops 12582912 | bytes 25165828 | tf_op jit(solution)/shard_map/div | solution.py:69
  (44 shorter events, 40.0 us)
Async XLA Ops:
  0.6 24.6 %copy-start.4 = (f32[2,512,512]{2,1,0:T(8,128)S(1)}, f32[2,512,512]{2,1,0:T(8,128)}, u32[]{:S(2)}) copy-start(f32[2,512,512]{2,1,0:T(8,128)} %param.5) | copy-start | bytes 6291460
  0.6 24.6 %copy-start = (f32[2,512,512]{2,1,0:T(8,128)S(1)}, f32[2,512,512]{2,1,0:T(8,128)}, u32[]{:S(2)}) copy-start(f32[2,512,512]{2,1,0:T(8,128)} %param.4) | copy-start | bytes 6291460
  2.5 21.5 %collective-permute-start = (f32[1,512,512]{2,1,0:T(8,128)S(1)}, f32[1,512,512]{2,1,0:T(8,128)S(1)}, u32[]{:S(2)}, u32[]{:S(2)}) collective-permute-start(f32[1,512,512]{2,1,0:T(8,128)S(1)} %get-tuple-element.35), channel_id=1, source_target_pairs={{1,0},{2,1},{3,2},{4,3},{5,4},{6,5},{7,6},{8,7},{9,8},{10,9},{11,1... | collective-permute-start | bytes 3145736 | tf_op jit(solution)/shard_map/ppermute | solution.py:24
  5.1 20.1 %collective-permute-start.1 = (f32[1,512,512]{2,1,0:T(8,128)S(1)}, f32[1,512,512]{2,1,0:T(8,128)S(1)}, u32[]{:S(2)}, u32[]{:S(2)}) collective-permute-start(f32[1,512,512]{2,1,0:T(8,128)S(1)} %get-tuple-element.36), channel_id=1, source_target_pairs={{0,1},{1,2},{2,3},{3,4},{4,5},{5,6},{6,7},{7,8},{8,9},{9,10},{10,1... | collective-permute-start | bytes 3145736 | tf_op jit(solution)/shard_map/ppermute | solution.py:23
  28.6 22.3 %collective-permute-start.2 = (f32[1,512,512]{2,1,0:T(8,128)S(1)}, f32[1,512,512]{2,1,0:T(8,128)S(1)}, u32[]{:S(2)}, u32[]{:S(2)}) collective-permute-start(f32[1,512,512]{2,1,0:T(8,128)S(1)} %get-tuple-element.33), channel_id=1, source_target_pairs={{1,0},{2,1},{3,2},{4,3},{5,4},{6,5},{7,6},{8,7},{9,8},{10,9},{11,1... | collective-permute-start | bytes 3145736 | tf_op jit(solution)/shard_map/ppermute | solution.py:24
  30.5 21.5 %collective-permute-start.3 = (f32[1,512,512]{2,1,0:T(8,128)S(1)}, f32[1,512,512]{2,1,0:T(8,128)S(1)}, u32[]{:S(2)}, u32[]{:S(2)}) collective-permute-start(f32[1,512,512]{2,1,0:T(8,128)S(1)} %get-tuple-element.34), channel_id=1, source_target_pairs={{0,1},{1,2},{2,3},{3,4},{4,5},{5,6},{6,7},{7,8},{8,9},{9,10},{10,1... | collective-permute-start | bytes 3145736 | tf_op jit(solution)/shard_map/ppermute | solution.py:23
  55.5 22.3 %collective-permute-start.4 = (f32[1,512,512]{2,1,0:T(8,128)S(1)}, f32[1,512,512]{2,1,0:T(8,128)S(1)}, u32[]{:S(2)}, u32[]{:S(2)}) collective-permute-start(f32[1,512,512]{2,1,0:T(8,128)S(1)} %get-tuple-element.31), channel_id=1, source_target_pairs={{1,0},{2,1},{3,2},{4,3},{5,4},{6,5},{7,6},{8,7},{9,8},{10,9},{11,1... | collective-permute-start | bytes 3145736 | tf_op jit(solution)/shard_map/ppermute | solution.py:24
  57.4 21.5 %collective-permute-start.5 = (f32[1,512,512]{2,1,0:T(8,128)S(1)}, f32[1,512,512]{2,1,0:T(8,128)S(1)}, u32[]{:S(2)}, u32[]{:S(2)}) collective-permute-start(f32[1,512,512]{2,1,0:T(8,128)S(1)} %get-tuple-element.32), channel_id=1, source_target_pairs={{0,1},{1,2},{2,3},{3,4},{4,5},{5,6},{6,7},{7,8},{8,9},{9,10},{10,1... | collective-permute-start | bytes 3145736 | tf_op jit(solution)/shard_map/ppermute | solution.py:23
  82.1 23.9 %copy-start.6 = (f32[2,512,512]{2,1,0:T(8,128)S(1)}, f32[2,512,512]{2,1,0:T(8,128)}, u32[]{:S(2)}) copy-start(f32[2,512,512]{2,1,0:T(8,128)} %param.6) | copy-start | bytes 6291460
  82.3 22.4 %collective-permute-start.6 = (f32[1,512,512]{2,1,0:T(8,128)S(1)}, f32[1,512,512]{2,1,0:T(8,128)S(1)}, u32[]{:S(2)}, u32[]{:S(2)}) collective-permute-start(f32[1,512,512]{2,1,0:T(8,128)S(1)} %get-tuple-element.29), channel_id=1, source_target_pairs={{1,0},{2,1},{3,2},{4,3},{5,4},{6,5},{7,6},{8,7},{9,8},{10,9},{11,1... | collective-permute-start | bytes 3145736 | tf_op jit(solution)/shard_map/ppermute | solution.py:24
  84.4 25.2 %copy-start.5 = (f32[2,512,512]{2,1,0:T(8,128)S(1)}, f32[2,512,512]{2,1,0:T(8,128)}, u32[]{:S(2)}) copy-start(f32[2,512,512]{2,1,0:T(8,128)} %param.7) | copy-start | bytes 6291460
  84.4 21.7 %collective-permute-start.7 = (f32[1,512,512]{2,1,0:T(8,128)S(1)}, f32[1,512,512]{2,1,0:T(8,128)S(1)}, u32[]{:S(2)}, u32[]{:S(2)}) collective-permute-start(f32[1,512,512]{2,1,0:T(8,128)S(1)} %get-tuple-element.30), channel_id=1, source_target_pairs={{0,1},{1,2},{2,3},{3,4},{4,5},{5,6},{6,7},{7,8},{8,9},{9,10},{10,1... | collective-permute-start | bytes 3145736 | tf_op jit(solution)/shard_map/ppermute | solution.py:23
  111.5 22.3 %collective-permute-start.8 = (f32[1,512,512]{2,1,0:T(8,128)S(1)}, f32[1,512,512]{2,1,0:T(8,128)S(1)}, u32[]{:S(2)}, u32[]{:S(2)}) collective-permute-start(f32[1,512,512]{2,1,0:T(8,128)S(1)} %get-tuple-element.27), channel_id=1, source_target_pairs={{1,0},{2,1},{3,2},{4,3},{5,4},{6,5},{7,6},{8,7},{9,8},{10,9},{11,1... | collective-permute-start | bytes 3145736 | tf_op jit(solution)/shard_map/ppermute | solution.py:24
  113.4 21.5 %collective-permute-start.9 = (f32[1,512,512]{2,1,0:T(8,128)S(1)}, f32[1,512,512]{2,1,0:T(8,128)S(1)}, u32[]{:S(2)}, u32[]{:S(2)}) collective-permute-start(f32[1,512,512]{2,1,0:T(8,128)S(1)} %get-tuple-element.28), channel_id=1, source_target_pairs={{0,1},{1,2},{2,3},{3,4},{4,5},{5,6},{6,7},{7,8},{8,9},{9,10},{10,1... | collective-permute-start | bytes 3145736 | tf_op jit(solution)/shard_map/ppermute | solution.py:23
  137.3 26.1 %copy-start.2 = (f32[2,512,512]{2,1,0:T(8,128)}, f32[2,512,512]{2,1,0:T(8,128)S(1)}, u32[]{:S(2)}) copy-start(f32[2,512,512]{2,1,0:T(8,128)S(1)} %get-tuple-element.10) | copy-start | bytes 6291460
  137.5 22.3 %collective-permute-start.10 = (f32[1,512,512]{2,1,0:T(8,128)S(1)}, f32[1,512,512]{2,1,0:T(8,128)S(1)}, u32[]{:S(2)}, u32[]{:S(2)}) collective-permute-start(f32[1,512,512]{2,1,0:T(8,128)S(1)} %get-tuple-element.25), channel_id=1, source_target_pairs={{1,0},{2,1},{3,2},{4,3},{5,4},{6,5},{7,6},{8,7},{9,8},{10,9},{11,1... | collective-permute-start | bytes 3145736 | tf_op jit(solution)/shard_map/ppermute | solution.py:24
  139.5 21.5 %collective-permute-start.11 = (f32[1,512,512]{2,1,0:T(8,128)S(1)}, f32[1,512,512]{2,1,0:T(8,128)S(1)}, u32[]{:S(2)}, u32[]{:S(2)}) collective-permute-start(f32[1,512,512]{2,1,0:T(8,128)S(1)} %get-tuple-element.26), channel_id=1, source_target_pairs={{0,1},{1,2},{2,3},{3,4},{4,5},{5,6},{6,7},{7,8},{8,9},{9,10},{10,1... | collective-permute-start | bytes 3145736 | tf_op jit(solution)/shard_map/ppermute | solution.py:23
  163.4 27.1 %copy-start.3 = (f32[2,512,512]{2,1,0:T(8,128)}, f32[2,512,512]{2,1,0:T(8,128)S(1)}, u32[]{:S(2)}) copy-start(f32[2,512,512]{2,1,0:T(8,128)S(1)} %get-tuple-element.8) | copy-start | bytes 6291460
  163.6 22.3 %collective-permute-start.12 = (f32[1,512,512]{2,1,0:T(8,128)S(1)}, f32[1,512,512]{2,1,0:T(8,128)S(1)}, u32[]{:S(2)}, u32[]{:S(2)}) collective-permute-start(f32[1,512,512]{2,1,0:T(8,128)S(1)} %get-tuple-element.23), channel_id=1, source_target_pairs={{1,0},{2,1},{3,2},{4,3},{5,4},{6,5},{7,6},{8,7},{9,8},{10,9},{11,1... | collective-permute-start | bytes 3145736 | tf_op jit(solution)/shard_map/ppermute | solution.py:24
  165.5 21.5 %collective-permute-start.13 = (f32[1,512,512]{2,1,0:T(8,128)S(1)}, f32[1,512,512]{2,1,0:T(8,128)S(1)}, u32[]{:S(2)}, u32[]{:S(2)}) collective-permute-start(f32[1,512,512]{2,1,0:T(8,128)S(1)} %get-tuple-element.24), channel_id=1, source_target_pairs={{0,1},{1,2},{2,3},{3,4},{4,5},{5,6},{6,7},{7,8},{8,9},{9,10},{10,1... | collective-permute-start | bytes 3145736 | tf_op jit(solution)/shard_map/ppermute | solution.py:23
  190.5 1.4 copy-start.1
  193.3 50.4 %collective-permute-start.14 = (f32[1,512,512]{2,1,0:T(8,128)}, f32[1,512,512]{2,1,0:T(8,128)S(1)}, u32[]{:S(2)}, u32[]{:S(2)}) collective-permute-start(f32[1,512,512]{2,1,0:T(8,128)} %get-tuple-element.21), channel_id=1, source_target_pairs={{1,0},{2,1},{3,2},{4,3},{5,4},{6,5},{7,6},{8,7},{9,8},{10,9},{11,1... | collective-permute-start | bytes 3145736 | tf_op jit(solution)/shard_map/ppermute | solution.py:24
  195.3 48.5 %collective-permute-start.15 = (f32[1,512,512]{2,1,0:T(8,128)}, f32[1,512,512]{2,1,0:T(8,128)}, u32[]{:S(2)}, u32[]{:S(2)}) collective-permute-start(f32[1,512,512]{2,1,0:T(8,128)} %get-tuple-element.22), channel_id=1, source_target_pairs={{0,1},{1,2},{2,3},{3,4},{4,5},{5,6},{6,7},{7,8},{8,9},{9,10},{10,1... | collective-permute-start | bytes 3145736 | tf_op jit(solution)/shard_map/ppermute | solution.py:23
where the time goes:
time: 262 us; the launch traced here: 258 us
  starting transfers between devices  93.6 us (36%)
  waiting for transfers between devices  81.9 us (31%)
  blocking collectives  38 us (15%)
  other arithmetic  36 us (14%)
  local copies, waits for them, and re-layouts  5.8 us (2%)
  between operations  2.72 us (1%)
    ppermute x8, starting transfers between devices, extended(): before = lax.ppermute(last, axis, up)  77.5 us
    ppermute x8, waiting for transfers between devices, extended(): after = lax.ppermute(initial, axis, down)  73.5 us
    psum x4, blocking collectives, by_axis(): return functools.reduce(lax.psum, axes, shard)  38 us
    ppermute x8, starting transfers between devices, extended(): after = lax.ppermute(initial, axis, down)  16.1 us
    div x1, other arithmetic, on_device(): adjoint = adjoint / misfit  13 us
    add x3, other arithmetic, on_device(): state = state + time_step * coefficient * slope  9.57 us
    mul x4, other arithmetic, on_device(): adjoint = adjoint + time_step * adjoint_slope(coefficient * adjoint)  8.62 us
    ppermute x8, waiting for transfers between devices, extended(): before = lax.ppermute(last, axis, up)  8.42 us
  transfers between devices with their start and end apart: 16, of which 14 were waited for; matrix products, arithmetic and copies ran while one was open for 0% of the time, Pallas kernels for 0%

commit v1 on v0

v1 whole, which is shorter than its diff:
```python
import functools

import jax
import jax.numpy as jnp
from jax import lax
from jax.experimental import pallas as pl
from jax.experimental.pallas import tpu as pltpu
from jax.sharding import PartitionSpec as P

MESH = pl.DeviceIdType.MESH
time_step = 0.125
ITERS = 4
CHUNKS = 8
PAD = 8
SUB, LANE = 8, 128


def kernel(
    n, ny, nx,
    c_hbm, u_hbm, o_hbm, w_hbm,
    grad_out, lam_out, tot_out,
    u, mu, slopes, c, o, w, lam, grad, ghost, part, incoming,
    load_sem, send_sem, recv_sem, tot_send, tot_recv, out_sem,
):
    me = lax.axis_index("gz")
    core = lax.rem(me, 2)
    beside = me + 1 - 2 * core
    beyond = me - 1 + 2 * core
    inner = jnp.logical_and(me > 0, me < n - 1)
    bits = n.bit_length() - 1
    partners = [me + (1 << b) - 2 * (1 << b) * lax.rem(me // (1 << b), 2) for b in range(bits)]
    rows = ny // CHUNKS
    tiles = nx // LANE

    planes = (core, 1 - core)
    loads = []
    for index, (source, target) in enumerate(((u_hbm, u), (c_hbm, c), (o_hbm, o), (w_hbm, w))):
        for slot in range(2):
            place = u.at[0, slot, pl.ds(PAD, ny), :] if target is u else target.at[slot]
            loads.append(pltpu.make_async_copy(source.at[planes[slot]], place, load_sem.at[index, slot]))
    for load in loads[:4]:
        load.start()

    barrier = pltpu.get_barrier_semaphore()
    for partner in partners:
        pl.semaphore_signal(barrier, inc=1, device_id=(partner,), device_id_type=MESH)

    @pl.when(inner)
    def _():
        pl.semaphore_signal(barrier, inc=1, device_id=(beyond,), device_id_type=MESH)

    pl.semaphore_wait(barrier, bits + inner.astype(jnp.int32))

    def copy_out(source, step, slot, start, count, target):
        return pltpu.make_async_remote_copy(
            src_ref=source,
            dst_ref=ghost.at[step, slot, pl.ds(start, count), :],
            send_sem=send_sem.at[step, slot],
            recv_sem=recv_sem.at[step, slot, start // rows],
            device_id=(target,),
            device_id_type=MESH,
        )

    def send(view, step, start):
        @pl.when(inner)
        def _():
            copy_out(view(0), step, 0, start, rows, beyond).start()

        copy_out(view(1), step, 1, start, rows, beside).start()

    def arrived(step, start):
        @pl.when(inner)
        def _():
            copy_out(ghost.at[step, 0, pl.ds(start, rows), :], step, 0, start, rows, beyond).wait_recv()

        copy_out(ghost.at[step, 1, pl.ds(start, rows), :], step, 1, start, rows, beside).wait_recv()

    for chunk in range(CHUNKS):
        start = chunk * rows
        send(lambda slot: u_hbm.at[planes[slot], pl.ds(start, rows), :], 0, start)
    for load in loads[4:]:
        load.start()

    edge = jnp.zeros((SUB, nx), jnp.float32)
    for field, count in ((u, ITERS), (mu, ITERS)):
        for step in range(count):
            for slot in range(2):
                field[step, slot, pl.ds(PAD - SUB, SUB), :] = edge
                field[step, slot, pl.ds(PAD + ny, SUB), :] = edge

    @pl.when(jnp.logical_not(inner))
    def _():
        def blank(at, carry):
            step, row = at // (ny // SUB), lax.rem(at, ny // SUB)
            ghost[step, 0, pl.ds(pl.multiple_of(row * SUB, SUB), SUB), :] = edge
            return carry

        lax.fori_loop(0, 2 * ITERS * (ny // SUB), blank, 0)

    sublane = lax.broadcasted_iota(jnp.int32, (SUB, LANE), 0)
    lane = lax.broadcasted_iota(jnp.int32, (SUB, LANE), 1)
    top, bottom = sublane == 0, sublane == SUB - 1
    first, last = lane == 0, lane == LANE - 1
    nothing = jnp.zeros((SUB, LANE), jnp.float32)

    def columns(tile):
        return pl.ds(tile * LANE, LANE)

    def laplace(field, step, halo, start, use):
        for slot in range(2):
            def row_of(at):
                at = pl.multiple_of(start + at + PAD, SUB)
                return [field[step, slot, pl.ds(at, SUB), columns(t)] for t in range(tiles)]

            above = [pltpu.roll(x, 1, 0) for x in row_of(-SUB)]
            here = row_of(0)
            here_down = [pltpu.roll(x, SUB - 1, 0) for x in here]
            for at in range(0, rows, SUB):
                below = row_of(at + SUB)
                below_down = [pltpu.roll(x, SUB - 1, 0) for x in below]
                here_up = [pltpu.roll(x, 1, 0) for x in here]
                right = [pltpu.roll(x, 1, 1) for x in here]
                left = [pltpu.roll(x, LANE - 1, 1) for x in here]
                row = pl.multiple_of(start + at, SUB)
                for t in range(tiles):
                    value = here[t]
                    beside_y = jnp.where(top, above[t], here_up[t]) + jnp.where(bottom, below_down[t], here_down[t])
                    before = jnp.where(first, right[t - 1] if t else nothing, right[t])
                    after = jnp.where(last, left[t + 1] if t < tiles - 1 else nothing, left[t])
                    other = field[step, 1 - slot, pl.ds(pl.multiple_of(row + PAD, SUB), SUB), columns(t)]
                    across = other + ghost[halo, slot, pl.ds(row, SUB), columns(t)]
                    lap = (across + beside_y + (before + after)) - 6.0 * value
                    use(slot, row, columns(t), value, lap)
                above, here, here_down = here_up, below, below_down

    for load in loads[:4]:
        load.wait()

    def forward(at, carry):
        step, chunk = at // CHUNKS, lax.rem(at, CHUNKS)
        start = pl.multiple_of(chunk * rows, rows)
        arrived(step, start)

        def use(slot, row, cols, value, lap):
            scaled = time_step * lap
            slopes[step, slot, pl.ds(row, SUB), cols] = scaled
            u[step + 1, slot, pl.ds(pl.multiple_of(row + PAD, SUB), SUB), cols] = (
                value + c[slot, pl.ds(row, SUB), cols] * scaled
            )

        laplace(u, step, step, start, use)
        send(lambda slot: u.at[step + 1, slot, pl.ds(start + PAD, rows), :], step + 1, start)
        return carry

    lax.fori_loop(0, (ITERS - 1) * CHUNKS, forward, 0)
    for load in loads[4:]:
        load.wait()
    part[0] = nothing

    def turn(chunk, carry):
        start = pl.multiple_of(chunk * rows, rows)
        arrived(ITERS - 1, start)
        sums = [nothing, nothing]

        def use(slot, row, cols, value, lap):
            scaled = time_step * lap
            at = (slot, pl.ds(row, SUB), cols)
            coefficient = c[at]
            resid = value + coefficient * scaled - o[at]
            adjoint = w[at] * resid
            sums[slot] = sums[slot] + adjoint * resid
            lam[at] = adjoint
            grad[at] = adjoint * scaled
            mu[0, slot, pl.ds(pl.multiple_of(row + PAD, SUB), SUB), cols] = coefficient * adjoint

        laplace(u, ITERS - 1, ITERS - 1, start, use)
        send(lambda slot: mu.at[0, slot, pl.ds(start + PAD, rows), :], ITERS, start)
        part[0] = part[0] + (sums[0] + sums[1])
        return carry

    lax.fori_loop(0, CHUNKS, turn, 0)

    def total_copy(bit):
        return pltpu.make_async_remote_copy(
            src_ref=part.at[bit],
            dst_ref=incoming.at[bit],
            send_sem=tot_send.at[bit],
            recv_sem=tot_recv.at[bit],
            device_id=(partners[bit],),
            device_id_type=MESH,
        )

    spacing = ITERS * CHUNKS // bits

    def total_step(bit):
        total_copy(bit).wait()
        part[bit + 1] = part[bit] + incoming[bit]

    def total_stages(at, low, high):
        for bit in range(bits):
            if low <= spacing * bit < high:
                @pl.when(at == spacing * bit)
                def _():
                    total_copy(bit).start()

            if low <= spacing * bit + spacing - 1 < high:
                @pl.when(at == spacing * bit + spacing - 1)
                def _():
                    total_step(bit)

    def adjoint(at, carry):
        step, chunk = at // CHUNKS, lax.rem(at, CHUNKS)
        start = pl.multiple_of(chunk * rows, rows)
        total_stages(at, 0, (ITERS - 1) * CHUNKS)
        arrived(ITERS + step, start)

        def use(slot, row, cols, value, lap):
            at = (slot, pl.ds(row, SUB), cols)
            fresh = lam[at] + time_step * lap
            lam[at] = fresh
            grad[at] = grad[at] + fresh * slopes[ITERS - 2 - step, slot, pl.ds(row, SUB), cols]
            mu[step + 1, slot, pl.ds(pl.multiple_of(row + PAD, SUB), SUB), cols] = c[at] * fresh

        laplace(mu, step, ITERS + step, start, use)
        send(lambda slot: mu.at[step + 1, slot, pl.ds(start + PAD, rows), :], ITERS + step + 1, start)
        return carry

    lax.fori_loop(0, (ITERS - 1) * CHUNKS, adjoint, 0)

    outs = [pltpu.make_async_copy(grad.at[slot], grad_out.at[planes[slot]], out_sem.at[0, slot]) for slot in range(2)]
    for out in outs:
        out.start()

    def lam_copy(slot, start, count):
        return pltpu.make_async_copy(
            lam.at[slot, pl.ds(start, count), :],
            lam_out.at[planes[slot], pl.ds(start, count), :],
            out_sem.at[1, slot],
        )

    def finish(chunk, carry):
        start = pl.multiple_of(chunk * rows, rows)
        total_stages(chunk + (ITERS - 1) * CHUNKS, (ITERS - 1) * CHUNKS, ITERS * CHUNKS)
        arrived(2 * ITERS - 1, start)

        def use(slot, row, cols, value, lap):
            at = (slot, pl.ds(row, SUB), cols)
            lam[at] = lam[at] + time_step * lap

        laplace(mu, ITERS - 1, 2 * ITERS - 1, start, use)
        for slot in range(2):
            lam_copy(slot, start, rows).start()
        return carry

    lax.fori_loop(0, CHUNKS, finish, 0)
    total = pltpu.make_async_copy(part.at[bits], tot_out, out_sem.at[2, 0])
    total.start()

    for step in range(2 * ITERS):
        def whole(slot):
            if step == 0:
                return u_hbm.at[planes[slot]]
            return (u.at[step, slot] if step < ITERS else mu.at[step - ITERS, slot]).at[pl.ds(PAD, ny), :]

        @pl.when(inner)
        def _():
            copy_out(whole(0), step, 0, 0, ny, beyond).wait_send()

        copy_out(whole(1), step, 1, 0, ny, beside).wait_send()
    for out in outs:
        out.wait()
    for slot in range(2):
        lam_copy(slot, 0, ny).wait()
    total.wait()


def on_device(n, coefficient, initial_field, observed, misfit_weight):
    depth, ny, nx = coefficient.shape
    bits = n.bit_length() - 1
    anywhere = pl.BlockSpec(memory_space=pl.ANY)
    slab = jax.ShapeDtypeStruct(coefficient.shape, jnp.float32)
    padded = (ITERS, depth, ny + 2 * PAD, nx)
    gradient, adjoint, tile = pl.pallas_call(
        functools.partial(kernel, n, ny, nx),
        out_shape=(slab, slab, jax.ShapeDtypeStruct((SUB, LANE), jnp.float32)),
        in_specs=[anywhere] * 4,
        out_specs=(anywhere,) * 3,
        scratch_shapes=[
            pltpu.VMEM(padded, jnp.float32),
            pltpu.VMEM(padded, jnp.float32),
            pltpu.VMEM((ITERS - 1, depth, ny, nx), jnp.float32),
            pltpu.VMEM((depth, ny, nx), jnp.float32),
            pltpu.VMEM((depth, ny, nx), jnp.float32),
            pltpu.VMEM((depth, ny, nx), jnp.float32),
            pltpu.VMEM((depth, ny, nx), jnp.float32),
            pltpu.VMEM((depth, ny, nx), jnp.float32),
            pltpu.VMEM((2 * ITERS, 2, ny, nx), jnp.float32),
            pltpu.VMEM((bits + 1, SUB, LANE), jnp.float32),
            pltpu.VMEM((bits, SUB, LANE), jnp.float32),
            pltpu.SemaphoreType.DMA((4, 2)),
            pltpu.SemaphoreType.DMA((2 * ITERS, 2)),
            pltpu.SemaphoreType.DMA((2 * ITERS, 2, CHUNKS)),
            pltpu.SemaphoreType.DMA((bits,)),
            pltpu.SemaphoreType.DMA((bits,)),
            pltpu.SemaphoreType.DMA((3, 2)),
        ],
        compiler_params=pltpu.CompilerParams(
            collective_id=0, has_side_effects=True, vmem_limit_bytes=60 * 1024 * 1024
        ),
    )(coefficient, initial_field, observed, misfit_weight)
    cells = n * depth * ny * nx
    misfit = jnp.sqrt(jnp.sum(tile) / cells + 1e-06)
    return gradient / misfit, adjoint / misfit, misfit


def solution(mesh):
    slab = P("gz", None, None)
    return jax.shard_map(
        functools.partial(on_device, mesh.shape["gz"]),
        mesh=mesh,
        in_specs=(slab,) * 4,
        out_specs=(slab, slab, P()),
        check_vma=False,
    )
```

time: 262 us -> 129 us (0.49)
  the two profiles are of different devices: /device:TPU:127 before, /device:TPU:6 now
where the time goes in v1:
time: 129 us
  Pallas kernels  120 us (93%)
  other arithmetic  6.03 us (5%)
  between operations  2.46 us (2%)
    pallas_call x1, Pallas kernels, on_device(): pl.pallas_call(functools.partial(kernel, n, ny, nx), out_shape=(slab, sla...  120 us
    div x1, other arithmetic, on_device(): return (gradient / misfit, adjoint / misfit, misfit)  4.74 us

profile of v1, /device:TPU:6, one launch (start us, length us, event | category | flops | bytes accessed | tf_op | source)
XLA Modules:
  0.0 128.8 jit_solution(5623551454925781882)
XLA Ops:
  0.6 120.3 %shard_map.67 = (f32[2,512,512]{2,1,0:T(8,128)}, f32[2,512,512]{2,1,0:T(8,128)}, f32[8,128]{1,0:T(8,128)}) custom-call(f32[2,512,512]{2,1,0:T(8,128)} %c_hbm.1, f32[2,512,512]{2,1,0:T(8,128)} %u_hbm.1, f32[2,512,512]{2,1,0:T(8,128)} %o_hbm.1, f32[2,512,512]{2,1,0:T(8,128)} %w_hbm.1), custom_call_target="tpu_custom_call" | custom-call | tf_op jit(solution)/shard_map/pallas_call | solution.py:283
  120.9 1.3 %reduce_sum.9 = f32[]{:T(128)} reduce(f32[8,128]{1,0:T(8,128)} %get-tuple-element.7, f32[]{:T(128)} %constant.1.clone.1), dimensions={0,1}, to_apply=%region_0.0 | reduce | flops 1023 | bytes 4104 | tf_op jit(solution)/shard_map/reduce_sum | solution.py:312
  122.9 4.7 %broadcast_divide_fusion = (f32[2,512,512]{2,1,0:T(8,128)}, f32[2,512,512]{2,1,0:T(8,128)}) fusion(f32[2,512,512]{2,1,0:T(8,128)} %get-tuple-element.8, f32[]{:T(128)} %sqrt.3, f32[2,512,512]{2,1,0:T(8,128)} %get-tuple-element.6), kind=kLoop, calls=%fused_computation | loop fusion | flops 1048576 | bytes 8388612 | tf_op jit(solution)/shard_map/div | solution.py:313

commit v2 on v1

--- a/solution.py
+++ b/solution.py
@@ -1,4 +1,6 @@
 import functools
+import itertools
+import math
 
 import jax
 import jax.numpy as jnp
@@ -13,13 +15,37 @@
 CHUNKS = 8
 PAD = 8
 SUB, LANE = 8, 128
+STAGE_TIMES = ((0, 12), (13, 21), (22, None))
+
+
+def stages(n):
+    x = min(4, n // 2)
+    y = min(4, n // (2 * x))
+    z = n // (2 * x * y)
+    return ((2, x),), ((2 * x, y), (1, 2)), ((2 * x * y, z),)
+
+
+def group_of(me, axes):
+    here, base, size = 0, me, math.prod(size for _, size in axes)
+    weights = [math.prod(size for _, size in axes[at + 1:]) for at in range(len(axes))]
+    places = [lax.rem(me // stride, size) for stride, size in axes]
+    for place, weight, (stride, _) in zip(places, weights, axes):
+        here, base = here + place * weight, base - place * stride
+    others = []
+    for turn in itertools.islice(itertools.product(*(range(size) for _, size in axes)), 1, None):
+        device, slot = base, 0
+        for place, step, weight, (stride, count) in zip(places, turn, weights, axes):
+            other = lax.rem(place + step, count)
+            device, slot = device + other * stride, slot + other * weight
+        others.append((device, slot))
+    return here, others
 
 
 def kernel(
     n, ny, nx,
     c_hbm, u_hbm, o_hbm, w_hbm,
     grad_out, lam_out, tot_out,
-    u, mu, slopes, c, o, w, lam, grad, ghost, part, incoming,
+    u, mu, slopes, c, o, w, lam, grad, ghost, tiles_of, total_of,
     load_sem, send_sem, recv_sem, tot_send, tot_recv, out_sem,
 ):
     me = lax.axis_index("gz")
@@ -27,8 +53,8 @@
     beside = me + 1 - 2 * core
     beyond = me - 1 + 2 * core
     inner = jnp.logical_and(me > 0, me < n - 1)
-    bits = n.bit_length() - 1
-    partners = [me + (1 << b) - 2 * (1 << b) * lax.rem(me // (1 << b), 2) for b in range(bits)]
+    groups = [group_of(me, axes) for axes in stages(n)]
+    partners = [device for _, others in groups for device, _ in others]
     rows = ny // CHUNKS
     tiles = nx // LANE
 
@@ -49,7 +75,7 @@
     def _():
         pl.semaphore_signal(barrier, inc=1, device_id=(beyond,), device_id_type=MESH)
 
-    pl.semaphore_wait(barrier, bits + inner.astype(jnp.int32))
+    pl.semaphore_wait(barrier, len(partners) + inner.astype(jnp.int32))
 
     def copy_out(source, step, slot, start, count, target):
         return pltpu.make_async_remote_copy(
@@ -155,7 +181,7 @@
     lax.fori_loop(0, (ITERS - 1) * CHUNKS, forward, 0)
     for load in loads[4:]:
         load.wait()
-    part[0] = nothing
+    total_of[...] = nothing
 
     def turn(chunk, carry):
         start = pl.multiple_of(chunk * rows, rows)
@@ -175,43 +201,63 @@
 
         laplace(u, ITERS - 1, ITERS - 1, start, use)
         send(lambda slot: mu.at[0, slot, pl.ds(start + PAD, rows), :], ITERS, start)
-        part[0] = part[0] + (sums[0] + sums[1])
+        total_of[...] = total_of[...] + (sums[0] + sums[1])
         return carry
 
     lax.fori_loop(0, CHUNKS, turn, 0)
 
-    def total_copy(bit):
+    def tile_copy(stage, device, slot):
+        here, _ = groups[stage]
         return pltpu.make_async_remote_copy(
-            src_ref=part.at[bit],
-            dst_ref=incoming.at[bit],
-            send_sem=tot_send.at[bit],
-            recv_sem=tot_recv.at[bit],
-            device_id=(partners[bit],),
+            src_ref=tiles_of.at[stage, here],
+            dst_ref=tiles_of.at[stage, here],
+            send_sem=tot_send.at[stage, slot],
+            recv_sem=tot_recv.at[stage, here],
+            device_id=(device,),
             device_id_type=MESH,
         )
 
-    spacing = ITERS * CHUNKS // bits
-
-    def total_step(bit):
-        total_copy(bit).wait()
-        part[bit + 1] = part[bit] + incoming[bit]
-
-    def total_stages(at, low, high):
-        for bit in range(bits):
-            if low <= spacing * bit < high:
-                @pl.when(at == spacing * bit)
+    def place(stage):
+        tiles_of[stage, groups[stage][0]] = total_of[...]
+
+    def exchange(stage):
+        for device, slot in groups[stage][1]:
+            tile_copy(stage, device, slot).start()
+
+    def collect(stage):
+        for device, slot in groups[stage][1]:
+            tile_copy(stage, device, slot).wait_send()
+            pltpu.make_async_remote_copy(
+                src_ref=tiles_of.at[stage, slot],
+                dst_ref=tiles_of.at[stage, slot],
+                send_sem=tot_send.at[stage, slot],
+                recv_sem=tot_recv.at[stage, slot],
+                device_id=(device,),
+                device_id_type=MESH,
+            ).wait_recv()
+        total = tiles_of[stage, 0]
+        for slot in range(1, len(groups[stage][1]) + 1):
+            total = total + tiles_of[stage, slot]
+        total_of[...] = total
+
+    place(0)
+
+    def total_stages(at):
+        for stage, (first_at, last_at) in enumerate(STAGE_TIMES):
+            @pl.when(at == first_at)
+            def _():
+                exchange(stage)
+
+            if stage < len(STAGE_TIMES) - 1:
+                @pl.when(at == last_at)
                 def _():
-                    total_copy(bit).start()
-
-            if low <= spacing * bit + spacing - 1 < high:
-                @pl.when(at == spacing * bit + spacing - 1)
-                def _():
-                    total_step(bit)
+                    collect(stage)
+                    place(stage + 1)
 
     def adjoint(at, carry):
         step, chunk = at // CHUNKS, lax.rem(at, CHUNKS)
         start = pl.multiple_of(chunk * rows, rows)
-        total_stages(at, 0, (ITERS - 1) * CHUNKS)
+        total_stages(at)
         arrived(ITERS + step, start)
 
         def use(slot, row, cols, value, lap):
@@ -240,7 +286,6 @@
 
     def finish(chunk, carry):
         start = pl.multiple_of(chunk * rows, rows)
-        total_stages(chunk + (ITERS - 1) * CHUNKS, (ITERS - 1) * CHUNKS, ITERS * CHUNKS)
         arrived(2 * ITERS - 1, start)
 
         def use(slot, row, cols, value, lap):
@@ -253,7 +298,8 @@
         return carry
 
     lax.fori_loop(0, CHUNKS, finish, 0)
-    total = pltpu.make_async_copy(part.at[bits], tot_out, out_sem.at[2, 0])
+    collect(len(groups) - 1)
+    total = pltpu.make_async_copy(total_of, tot_out, out_sem.at[2, 0])
     total.start()
 
     for step in range(2 * ITERS):
@@ -276,7 +322,8 @@
 
 def on_device(n, coefficient, initial_field, observed, misfit_weight):
     depth, ny, nx = coefficient.shape
-    bits = n.bit_length() - 1
+    groups = stages(n)
+    most = max(math.prod(size for _, size in axes) for axes in groups)
     anywhere = pl.BlockSpec(memory_space=pl.ANY)
     slab = jax.ShapeDtypeStruct(coefficient.shape, jnp.float32)
     padded = (ITERS, depth, ny + 2 * PAD, nx)
@@ -295,13 +342,13 @@
             pltpu.VMEM((depth, ny, nx), jnp.float32),
             pltpu.VMEM((depth, ny, nx), jnp.float32),
             pltpu.VMEM((2 * ITERS, 2, ny, nx), jnp.float32),
-            pltpu.VMEM((bits + 1, SUB, LANE), jnp.float32),
-            pltpu.VMEM((bits, SUB, LANE), jnp.float32),
+            pltpu.VMEM((len(groups), most, SUB, LANE), jnp.float32),
+            pltpu.VMEM((SUB, LANE), jnp.float32),
             pltpu.SemaphoreType.DMA((4, 2)),
             pltpu.SemaphoreType.DMA((2 * ITERS, 2)),
             pltpu.SemaphoreType.DMA((2 * ITERS, 2, CHUNKS)),
-            pltpu.SemaphoreType.DMA((bits,)),
-            pltpu.SemaphoreType.DMA((bits,)),
+            pltpu.SemaphoreType.DMA((len(groups), most)),
+            pltpu.SemaphoreType.DMA((len(groups), most)),
             pltpu.SemaphoreType.DMA((3, 2)),
         ],
         compiler_params=pltpu.CompilerParams(

time: 129 us -> 119 us (0.922)
  the two profiles are of different devices: /device:TPU:6 before, /device:TPU:127 now
where the time goes in v2:
time: 119 us; the launch traced here: 117 us
  Pallas kernels  108 us (91%)
  other arithmetic  6.03 us (5%)
  between operations  2.46 us (2%)
    pallas_call x1, Pallas kernels, on_device(): pl.pallas_call(functools.partial(kernel, n, ny, nx), out_shape=(slab, sla...  108 us
    div x1, other arithmetic, on_device(): return (gradient / misfit, adjoint / misfit, misfit)  4.74 us

profile of v2, /device:TPU:127, one launch (start us, length us, event | category | flops | bytes accessed | tf_op | source)
XLA Modules:
  0.0 116.9 jit_solution(15410337273694877824)
XLA Ops:
  0.6 108.4 %shard_map.67 = (f32[2,512,512]{2,1,0:T(8,128)}, f32[2,512,512]{2,1,0:T(8,128)}, f32[8,128]{1,0:T(8,128)}) custom-call(f32[2,512,512]{2,1,0:T(8,128)} %c_hbm.1, f32[2,512,512]{2,1,0:T(8,128)} %u_hbm.1, f32[2,512,512]{2,1,0:T(8,128)} %o_hbm.1, f32[2,512,512]{2,1,0:T(8,128)} %w_hbm.1), custom_call_target="tpu_custom_call" | custom-call | tf_op jit(solution)/shard_map/pallas_call | solution.py:330
  109.1 1.3 %reduce_sum.9 = f32[]{:T(128)} reduce(f32[8,128]{1,0:T(8,128)} %get-tuple-element.7, f32[]{:T(128)} %constant.1.clone.1), dimensions={0,1}, to_apply=%region_0.0 | reduce | flops 1023 | bytes 4104 | tf_op jit(solution)/shard_map/reduce_sum | solution.py:359
  111.0 4.7 %broadcast_divide_fusion = (f32[2,512,512]{2,1,0:T(8,128)}, f32[2,512,512]{2,1,0:T(8,128)}) fusion(f32[2,512,512]{2,1,0:T(8,128)} %get-tuple-element.8, f32[]{:T(128)} %sqrt.3, f32[2,512,512]{2,1,0:T(8,128)} %get-tuple-element.6), kind=kLoop, calls=%fused_computation | loop fusion | flops 1048576 | bytes 8388612 | tf_op jit(solution)/shard_map/div | solution.py:360

commit v3 on v1

--- a/solution.py
+++ b/solution.py
@@ -13,22 +13,54 @@
 CHUNKS = 8
 PAD = 8
 SUB, LANE = 8, 128
+PAIRS = 5
+STAGE_TIMES = ((0, 2), (3, 6), (7, 10), (11, 14), (15, 18), (19, None))
+HELLO_TIMES = (2, 8, 14, 20)
+
+
+def torus(n):
+    x = min(4, n // 2)
+    y = min(4, n // (2 * x))
+    return x, y, n // (2 * x * y)
 
 
 def kernel(
     n, ny, nx,
     c_hbm, u_hbm, o_hbm, w_hbm,
     grad_out, lam_out, tot_out,
-    u, mu, slopes, c, o, w, lam, grad, ghost, part, incoming,
-    load_sem, send_sem, recv_sem, tot_send, tot_recv, out_sem,
+    u, mu, slopes, c, o, w, lam, grad, ghost, totals, inbox, layers,
+    load_sem, send_sem, recv_sem, tot_send, tot_recv, out_sem, hello,
 ):
     me = lax.axis_index("gz")
     core = lax.rem(me, 2)
     beside = me + 1 - 2 * core
     beyond = me - 1 + 2 * core
     inner = jnp.logical_and(me > 0, me < n - 1)
-    bits = n.bit_length() - 1
-    partners = [me + (1 << b) - 2 * (1 << b) * lax.rem(me // (1 << b), 2) for b in range(bits)]
+    x, y, z = torus(n)
+    layer = 2 * x * y
+    row, column, depth = lax.rem(me // (2 * x), y), lax.rem(me // 2, x), me // layer
+    line = me - 2 * column - core
+
+    def chip_x(step):
+        return line + 2 * lax.rem(column + step % x, x)
+
+    def chip_y(step):
+        return me + 2 * x * (lax.rem(row + step % y, y) - row)
+
+    x_steps = sorted({1 % x, -1 % x} - {0})
+    y_steps = sorted({1 % y, -1 % y} - {0})
+    partners = [beside] + [chip_x(step) + c for step in x_steps for c in range(2)] + [chip_y(step) for step in y_steps]
+    line_end = jnp.logical_and(inner, jnp.where(core == 0, column == 0, column == x - 1))
+    reach = [step for step in (1, 2, 4) if step < z]
+
+    def along_z(step, act):
+        for away in (step, -step):
+            @pl.when(jnp.logical_and(depth + away >= 0, depth + away < z))
+            def _():
+                act(me + away * layer)
+
+        return (depth >= step).astype(jnp.int32) + (depth + step < z).astype(jnp.int32)
+
     rows = ny // CHUNKS
     tiles = nx // LANE
 
@@ -45,11 +77,15 @@
     for partner in partners:
         pl.semaphore_signal(barrier, inc=1, device_id=(partner,), device_id_type=MESH)
 
-    @pl.when(inner)
+    def ready(device):
+        pl.semaphore_signal(barrier, inc=1, device_id=(device,), device_id_type=MESH)
+
+    @pl.when(line_end)
     def _():
-        pl.semaphore_signal(barrier, inc=1, device_id=(beyond,), device_id_type=MESH)
-
-    pl.semaphore_wait(barrier, bits + inner.astype(jnp.int32))
+        ready(beyond)
+
+    others = along_z(1, ready) if reach else 0
+    pl.semaphore_wait(barrier, len(partners) + line_end.astype(jnp.int32) + others)
 
     def copy_out(source, step, slot, start, count, target):
         return pltpu.make_async_remote_copy(
@@ -136,7 +172,19 @@
     for load in loads[:4]:
         load.wait()
 
+    def greet(at):
+        for turn in range(len(reach) + 1):
+            @pl.when(at == HELLO_TIMES[turn])
+            def _():
+                if turn > 0:
+                    pl.semaphore_wait(hello.at[turn - 1], along_z(reach[turn - 1], lambda device: None))
+                if turn < len(reach):
+                    along_z(reach[turn], lambda device: pl.semaphore_signal(
+                        hello.at[turn], inc=1, device_id=(device,), device_id_type=MESH
+                    ))
+
     def forward(at, carry):
+        greet(at)
         step, chunk = at // CHUNKS, lax.rem(at, CHUNKS)
         start = pl.multiple_of(chunk * rows, rows)
         arrived(step, start)
@@ -155,7 +203,7 @@
     lax.fori_loop(0, (ITERS - 1) * CHUNKS, forward, 0)
     for load in loads[4:]:
         load.wait()
-    part[0] = nothing
+    totals[0] = nothing
 
     def turn(chunk, carry):
         start = pl.multiple_of(chunk * rows, rows)
@@ -175,43 +223,97 @@
 
         laplace(u, ITERS - 1, ITERS - 1, start, use)
         send(lambda slot: mu.at[0, slot, pl.ds(start + PAD, rows), :], ITERS, start)
-        part[0] = part[0] + (sums[0] + sums[1])
+        totals[0] = totals[0] + (sums[0] + sums[1])
         return carry
 
     lax.fori_loop(0, CHUNKS, turn, 0)
 
-    def total_copy(bit):
+    def tile_copy(source, target, stage, slot, device):
         return pltpu.make_async_remote_copy(
-            src_ref=part.at[bit],
-            dst_ref=incoming.at[bit],
-            send_sem=tot_send.at[bit],
-            recv_sem=tot_recv.at[bit],
-            device_id=(partners[bit],),
+            src_ref=source,
+            dst_ref=target,
+            send_sem=tot_send.at[stage, slot],
+            recv_sem=tot_recv.at[stage, slot],
+            device_id=(device,),
             device_id_type=MESH,
         )
 
-    spacing = ITERS * CHUNKS // bits
-
-    def total_step(bit):
-        total_copy(bit).wait()
-        part[bit + 1] = part[bit] + incoming[bit]
-
-    def total_stages(at, low, high):
-        for bit in range(bits):
-            if low <= spacing * bit < high:
-                @pl.when(at == spacing * bit)
+    def pair_copy(stage, device, slot=0):
+        return tile_copy(totals.at[stage], inbox.at[stage], stage, slot, device)
+
+    def pair_sends(stage, act):
+        if stage == 0:
+            act(pair_copy(0, beside))
+        elif stage < 3:
+            upper = lax.rem(column + stage - 1, 2) == 1
+            for step, sender in ((1, 0), (-1, 1)):
+                @pl.when(jnp.logical_and(core == sender, upper == (step == -1)))
                 def _():
-                    total_copy(bit).start()
-
-            if low <= spacing * bit + spacing - 1 < high:
-                @pl.when(at == spacing * bit + spacing - 1)
+                    for c in range(2):
+                        act(tile_copy(totals.at[stage], inbox.at[stage], stage, c, chip_x(step) + c))
+        else:
+            upper = lax.rem(row + stage - 3, 2) == 1
+            act(pair_copy(stage, jnp.where(upper, chip_y(-1), chip_y(1))))
+
+    def pair_there(stage):
+        return stage == 0 or (x, x // 2, y, y // 2)[stage - 1] > 1
+
+    def layer_copies(act):
+        for step in range(1, z):
+            device = lax.rem(depth + step, z) * layer + lax.rem(me, layer)
+            act(step, device)
+
+    def exchange(stage):
+        if stage < PAIRS:
+            if pair_there(stage):
+                pair_sends(stage, lambda copy: copy.start())
+        else:
+            def start(step, device):
+                tile_copy(layers.at[depth], layers.at[depth], stage, step, device).start()
+
+            layer_copies(start)
+
+    def collect(stage):
+        if stage < PAIRS:
+            if not pair_there(stage):
+                totals[stage + 1] = totals[stage]
+                return
+            pair_sends(stage, lambda copy: copy.wait_send())
+            if 0 < stage < 3:
+                for c in range(2):
+                    @pl.when(core == c)
+                    def _():
+                        pair_copy(stage, beside, c).wait_recv()
+            else:
+                pair_copy(stage, beside).wait_recv()
+            totals[stage + 1] = totals[stage] + inbox[stage]
+        else:
+            def finish(step, device):
+                tile_copy(layers.at[depth], layers.at[depth], stage, step, device).wait()
+
+            layer_copies(finish)
+            total = layers[0]
+            for slot in range(1, z):
+                total = total + layers[slot]
+            totals[stage + 1] = total
+
+    def total_stages(at):
+        for stage, (first_at, last_at) in enumerate(STAGE_TIMES):
+            @pl.when(at == first_at)
+            def _():
+                exchange(stage)
+
+            if stage < PAIRS:
+                @pl.when(at == last_at)
                 def _():
-                    total_step(bit)
+                    collect(stage)
+                    if stage == PAIRS - 1:
+                        layers[depth] = totals[PAIRS]
 
     def adjoint(at, carry):
         step, chunk = at // CHUNKS, lax.rem(at, CHUNKS)
         start = pl.multiple_of(chunk * rows, rows)
-        total_stages(at, 0, (ITERS - 1) * CHUNKS)
+        total_stages(at)
         arrived(ITERS + step, start)
 
         def use(slot, row, cols, value, lap):
@@ -240,7 +342,6 @@
 
     def finish(chunk, carry):
         start = pl.multiple_of(chunk * rows, rows)
-        total_stages(chunk + (ITERS - 1) * CHUNKS, (ITERS - 1) * CHUNKS, ITERS * CHUNKS)
         arrived(2 * ITERS - 1, start)
 
         def use(slot, row, cols, value, lap):
@@ -253,7 +354,8 @@
         return carry
 
     lax.fori_loop(0, CHUNKS, finish, 0)
-    total = pltpu.make_async_copy(part.at[bits], tot_out, out_sem.at[2, 0])
+    collect(PAIRS)
+    total = pltpu.make_async_copy(totals.at[PAIRS + 1], tot_out, out_sem.at[2, 0])
     total.start()
 
     for step in range(2 * ITERS):
@@ -276,7 +378,7 @@
 
 def on_device(n, coefficient, initial_field, observed, misfit_weight):
     depth, ny, nx = coefficient.shape
-    bits = n.bit_length() - 1
+    layers = torus(n)[2]
     anywhere = pl.BlockSpec(memory_space=pl.ANY)
     slab = jax.ShapeDtypeStruct(coefficient.shape, jnp.float32)
     padded = (ITERS, depth, ny + 2 * PAD, nx)
@@ -295,14 +397,16 @@
             pltpu.VMEM((depth, ny, nx), jnp.float32),
             pltpu.VMEM((depth, ny, nx), jnp.float32),
             pltpu.VMEM((2 * ITERS, 2, ny, nx), jnp.float32),
-            pltpu.VMEM((bits + 1, SUB, LANE), jnp.float32),
-            pltpu.VMEM((bits, SUB, LANE), jnp.float32),
+            pltpu.VMEM((PAIRS + 2, SUB, LANE), jnp.float32),
+            pltpu.VMEM((PAIRS, SUB, LANE), jnp.float32),
+            pltpu.VMEM((layers, SUB, LANE), jnp.float32),
             pltpu.SemaphoreType.DMA((4, 2)),
             pltpu.SemaphoreType.DMA((2 * ITERS, 2)),
             pltpu.SemaphoreType.DMA((2 * ITERS, 2, CHUNKS)),
-            pltpu.SemaphoreType.DMA((bits,)),
-            pltpu.SemaphoreType.DMA((bits,)),
+            pltpu.SemaphoreType.DMA((PAIRS + 1, max(layers, 2))),
+            pltpu.SemaphoreType.DMA((PAIRS + 1, max(layers, 2))),
             pltpu.SemaphoreType.DMA((3, 2)),
+            pltpu.SemaphoreType.REGULAR((3,)),
         ],
         compiler_params=pltpu.CompilerParams(
             collective_id=0, has_side_effects=True, vmem_limit_bytes=60 * 1024 * 1024

time: 129 us -> 111 us (0.86)
  the two profiles are of different devices: /device:TPU:6 before, /device:TPU:127 now
where the time goes in v3:
time: 111 us
  Pallas kernels  103 us (93%)
  other arithmetic  6.03 us (5%)
  between operations  2.46 us (2%)
    pallas_call x1, Pallas kernels, on_device(): pl.pallas_call(functools.partial(kernel, n, ny, nx), out_shape=(slab, sla...  103 us
    div x1, other arithmetic, on_device(): return (gradient / misfit, adjoint / misfit, misfit)  4.74 us

profile of v3, /device:TPU:127, one launch (start us, length us, event | category | flops | bytes accessed | tf_op | source)
XLA Modules:
  0.0 111.0 jit_solution(8879397036245229725)
XLA Ops:
  0.6 102.6 %shard_map.67 = (f32[2,512,512]{2,1,0:T(8,128)}, f32[2,512,512]{2,1,0:T(8,128)}, f32[8,128]{1,0:T(8,128)}) custom-call(f32[2,512,512]{2,1,0:T(8,128)} %c_hbm.1, f32[2,512,512]{2,1,0:T(8,128)} %u_hbm.1, f32[2,512,512]{2,1,0:T(8,128)} %o_hbm.1, f32[2,512,512]{2,1,0:T(8,128)} %w_hbm.1), custom_call_target="tpu_custom_call" | custom-call | tf_op jit(solution)/shard_map/pallas_call | solution.py:385
  103.2 1.3 %reduce_sum.9 = f32[]{:T(128)} reduce(f32[8,128]{1,0:T(8,128)} %get-tuple-element.7, f32[]{:T(128)} %constant.1.clone.1), dimensions={0,1}, to_apply=%region_0.0 | reduce | flops 1023 | bytes 4104 | tf_op jit(solution)/shard_map/reduce_sum | solution.py:416
  105.2 4.7 %broadcast_divide_fusion = (f32[2,512,512]{2,1,0:T(8,128)}, f32[2,512,512]{2,1,0:T(8,128)}) fusion(f32[2,512,512]{2,1,0:T(8,128)} %get-tuple-element.8, f32[]{:T(128)} %sqrt.3, f32[2,512,512]{2,1,0:T(8,128)} %get-tuple-element.6), kind=kLoop, calls=%fused_computation | loop fusion | flops 1048576 | bytes 8388612 | tf_op jit(solution)/shard_map/div | solution.py:417

commit v4 on v3

--- a/solution.py
+++ b/solution.py
@@ -13,6 +13,7 @@
 CHUNKS = 8
 PAD = 8
 SUB, LANE = 8, 128
+PIECES = 4
 PAIRS = 5
 STAGE_TIMES = ((0, 2), (3, 6), (7, 10), (11, 14), (15, 18), (19, None))
 HELLO_TIMES = (2, 8, 14, 20)
@@ -27,9 +28,9 @@
 def kernel(
     n, ny, nx,
     c_hbm, u_hbm, o_hbm, w_hbm,
-    grad_out, lam_out, tot_out,
-    u, mu, slopes, c, o, w, lam, grad, ghost, totals, inbox, layers,
-    load_sem, send_sem, recv_sem, tot_send, tot_recv, out_sem, hello,
+    grad, lam, tot_out,
+    u, mu, slopes, c, o, w, ghost, totals, inbox, layers,
+    load_sem, send_sem, recv_sem, tot_send, tot_recv, hello,
 ):
     me = lax.axis_index("gz")
     core = lax.rem(me, 2)
@@ -329,17 +330,6 @@
 
     lax.fori_loop(0, (ITERS - 1) * CHUNKS, adjoint, 0)
 
-    outs = [pltpu.make_async_copy(grad.at[slot], grad_out.at[planes[slot]], out_sem.at[0, slot]) for slot in range(2)]
-    for out in outs:
-        out.start()
-
-    def lam_copy(slot, start, count):
-        return pltpu.make_async_copy(
-            lam.at[slot, pl.ds(start, count), :],
-            lam_out.at[planes[slot], pl.ds(start, count), :],
-            out_sem.at[1, slot],
-        )
-
     def finish(chunk, carry):
         start = pl.multiple_of(chunk * rows, rows)
         arrived(2 * ITERS - 1, start)
@@ -349,14 +339,11 @@
             lam[at] = lam[at] + time_step * lap
 
         laplace(mu, ITERS - 1, 2 * ITERS - 1, start, use)
-        for slot in range(2):
-            lam_copy(slot, start, rows).start()
         return carry
 
     lax.fori_loop(0, CHUNKS, finish, 0)
     collect(PAIRS)
-    total = pltpu.make_async_copy(totals.at[PAIRS + 1], tot_out, out_sem.at[2, 0])
-    total.start()
+    tot_out[...] = totals[PAIRS + 1]
 
     for step in range(2 * ITERS):
         def whole(slot):
@@ -369,30 +356,48 @@
             copy_out(whole(0), step, 0, 0, ny, beyond).wait_send()
 
         copy_out(whole(1), step, 1, 0, ny, beside).wait_send()
-    for out in outs:
-        out.wait()
-    for slot in range(2):
-        lam_copy(slot, 0, ny).wait()
-    total.wait()
+
+
+def scale_kernel(cells, grad, lam, tile, grad_out, lam_out, misfit_out, scaled_grad, scaled_lam, out_sem):
+    core = lax.rem(lax.axis_index("gz"), 2)
+    ny = grad.shape[1]
+    rows = ny // PIECES
+    misfit = jnp.sqrt(jnp.sum(tile[...], keepdims=True) / cells + 1e-06)
+    factor = 1.0 / misfit
+    copies = []
+    for which, (source, scaled, target) in enumerate(((grad, scaled_grad, grad_out), (lam, scaled_lam, lam_out))):
+        for slot in range(2):
+            for piece in range(PIECES):
+                part = pl.ds(piece * rows, rows)
+                scaled[slot, part, :] = source[slot, part, :] * factor
+                plane = core if slot == 0 else 1 - core
+                copies.append(
+                    pltpu.make_async_copy(
+                        scaled.at[slot, part, :], target.at[plane, part, :], out_sem.at[which, slot, piece]
+                    )
+                )
+                copies[-1].start()
+    misfit_out[0, 0] = misfit[0, 0]
+    for copy in copies:
+        copy.wait()
 
 
 def on_device(n, coefficient, initial_field, observed, misfit_weight):
     depth, ny, nx = coefficient.shape
     layers = torus(n)[2]
-    anywhere = pl.BlockSpec(memory_space=pl.ANY)
+    far = pl.BlockSpec(memory_space=pltpu.HBM)
+    near = pl.BlockSpec(memory_space=pltpu.VMEM)
     slab = jax.ShapeDtypeStruct(coefficient.shape, jnp.float32)
     padded = (ITERS, depth, ny + 2 * PAD, nx)
     gradient, adjoint, tile = pl.pallas_call(
         functools.partial(kernel, n, ny, nx),
         out_shape=(slab, slab, jax.ShapeDtypeStruct((SUB, LANE), jnp.float32)),
-        in_specs=[anywhere] * 4,
-        out_specs=(anywhere,) * 3,
+        in_specs=[far] * 4,
+        out_specs=(near,) * 3,
         scratch_shapes=[
             pltpu.VMEM(padded, jnp.float32),
             pltpu.VMEM(padded, jnp.float32),
             pltpu.VMEM((ITERS - 1, depth, ny, nx), jnp.float32),
-            pltpu.VMEM((depth, ny, nx), jnp.float32),
-            pltpu.VMEM((depth, ny, nx), jnp.float32),
             pltpu.VMEM((depth, ny, nx), jnp.float32),
             pltpu.VMEM((depth, ny, nx), jnp.float32),
             pltpu.VMEM((depth, ny, nx), jnp.float32),
@@ -405,16 +410,25 @@
             pltpu.SemaphoreType.DMA((2 * ITERS, 2, CHUNKS)),
             pltpu.SemaphoreType.DMA((PAIRS + 1, max(layers, 2))),
             pltpu.SemaphoreType.DMA((PAIRS + 1, max(layers, 2))),
-            pltpu.SemaphoreType.DMA((3, 2)),
             pltpu.SemaphoreType.REGULAR((3,)),
         ],
         compiler_params=pltpu.CompilerParams(
-            collective_id=0, has_side_effects=True, vmem_limit_bytes=60 * 1024 * 1024
+            collective_id=0, has_side_effects=True, vmem_limit_bytes=48 * 1024 * 1024
         ),
     )(coefficient, initial_field, observed, misfit_weight)
-    cells = n * depth * ny * nx
-    misfit = jnp.sqrt(jnp.sum(tile) / cells + 1e-06)
-    return gradient / misfit, adjoint / misfit, misfit
+    gradient, adjoint, misfit = pl.pallas_call(
+        functools.partial(scale_kernel, n * depth * ny * nx),
+        out_shape=(slab, slab, jax.ShapeDtypeStruct((1, 1), jnp.float32)),
+        in_specs=[near] * 3,
+        out_specs=(far, far, pl.BlockSpec(memory_space=pltpu.SMEM)),
+        scratch_shapes=[
+            pltpu.VMEM((depth, ny, nx), jnp.float32),
+            pltpu.VMEM((depth, ny, nx), jnp.float32),
+            pltpu.SemaphoreType.DMA((2, 2, PIECES)),
+        ],
+        compiler_params=pltpu.CompilerParams(vmem_limit_bytes=8 * 1024 * 1024),
+    )(gradient, adjoint, tile)
+    return gradient, adjoint, misfit.reshape(())
 
 
 def solution(mesh):

time: 111 us -> 105 us (0.946)
  other arithmetic: 6.03 us -> 0 us
  Pallas kernels: 103 us -> 105 us
  between operations: 2.46 us -> 0.64 us
    div x1 -> x0, other arithmetic: 4.74 us -> none  [on_device(): return (gradient / misfit, adjoint / misfit, misfit)]
    pallas_call x0 -> x1, Pallas kernels: none -> 2.8 us  [on_device(): pl.pallas_call(functools.partial(scale_kernel, n * depth * ny * nx), out_...]
    reduce_sum x1 -> x0, other arithmetic: 1.29 us -> none  [on_device(): misfit = jnp.sqrt(jnp.sum(tile) / cells + 1e-06)]
where the time goes in v4:
time: 105 us
  Pallas kernels  105 us (100%)
    pallas_call x1, Pallas kernels, on_device(): pl.pallas_call(functools.partial(kernel, n, ny, nx), out_shape=(slab, sla...  102 us
    pallas_call x1, Pallas kernels, on_device(): pl.pallas_call(functools.partial(scale_kernel, n * depth * ny * nx), out_...  2.8 us

profile of v4, /device:TPU:127, one launch (start us, length us, event | category | flops | bytes accessed | tf_op | source)
XLA Modules:
  0.0 105.3 jit_solution(423433592411975451)
XLA Ops:
  0.6 101.9 %shard_map.67 = (f32[2,512,512]{2,1,0:T(8,128)S(1)}, f32[2,512,512]{2,1,0:T(8,128)S(1)}, f32[8,128]{1,0:T(8,128)S(1)}) custom-call(f32[2,512,512]{2,1,0:T(8,128)} %c_hbm.1, f32[2,512,512]{2,1,0:T(8,128)} %u_hbm.1, f32[2,512,512]{2,1,0:T(8,128)} %o_hbm.1, f32[2,512,512]{2,1,0:T(8,128)} %w_hbm.1), custom_call_target="tpu_custom_call" | custom-call | tf_op jit(solution)/shard_map/pallas_call | solution.py:392
  102.5 2.8 %shard_map.68 = (f32[2,512,512]{2,1,0:T(8,128)}, f32[2,512,512]{2,1,0:T(8,128)}, f32[1,1]{1,0:T(1,128)}) custom-call(f32[2,512,512]{2,1,0:T(8,128)S(1)} %get-tuple-element.9.grad, f32[2,512,512]{2,1,0:T(8,128)S(1)} %get-tuple-element.10.lam, f32[8,128]{1,0:T(8,128)S(1)} %get-tuple-element.11.tile), custom_call_target="tpu_custom_call" | custom-call | tf_op jit(solution)/shard_map/pallas_call | solution.py:419

commit v5 on v4

--- a/solution.py
+++ b/solution.py
@@ -13,7 +13,7 @@
 CHUNKS = 8
 PAD = 8
 SUB, LANE = 8, 128
-PIECES = 4
+SUM_CHUNK = 5
 PAIRS = 5
 STAGE_TIMES = ((0, 2), (3, 6), (7, 10), (11, 14), (15, 18), (19, None))
 HELLO_TIMES = (2, 8, 14, 20)
@@ -28,9 +28,9 @@
 def kernel(
     n, ny, nx,
     c_hbm, u_hbm, o_hbm, w_hbm,
-    grad, lam, tot_out,
+    grad, lam, misfit_out,
     u, mu, slopes, c, o, w, ghost, totals, inbox, layers,
-    load_sem, send_sem, recv_sem, tot_send, tot_recv, hello,
+    load_sem, send_sem, recv_sem, tot_send, tot_recv, layer_send, layer_recv, hello,
 ):
     me = lax.axis_index("gz")
     core = lax.rem(me, 2)
@@ -71,12 +71,7 @@
         for slot in range(2):
             place = u.at[0, slot, pl.ds(PAD, ny), :] if target is u else target.at[slot]
             loads.append(pltpu.make_async_copy(source.at[planes[slot]], place, load_sem.at[index, slot]))
-    for load in loads[:4]:
-        load.start()
-
     barrier = pltpu.get_barrier_semaphore()
-    for partner in partners:
-        pl.semaphore_signal(barrier, inc=1, device_id=(partner,), device_id_type=MESH)
 
     def ready(device):
         pl.semaphore_signal(barrier, inc=1, device_id=(device,), device_id_type=MESH)
@@ -85,7 +80,13 @@
     def _():
         ready(beyond)
 
+    for partner in partners:
+        ready(partner)
     others = along_z(1, ready) if reach else 0
+    for load in loads[:4]:
+        load.start()
+    for load in loads[:2]:
+        load.wait()
     pl.semaphore_wait(barrier, len(partners) + line_end.astype(jnp.int32) + others)
 
     def copy_out(source, step, slot, start, count, target):
@@ -93,7 +94,7 @@
             src_ref=source,
             dst_ref=ghost.at[step, slot, pl.ds(start, count), :],
             send_sem=send_sem.at[step, slot],
-            recv_sem=recv_sem.at[step, slot, start // rows],
+            recv_sem=recv_sem.at[step % 2 if isinstance(step, int) else lax.rem(step, 2), slot, start // rows],
             device_id=(target,),
             device_id_type=MESH,
         )
@@ -114,7 +115,7 @@
 
     for chunk in range(CHUNKS):
         start = chunk * rows
-        send(lambda slot: u_hbm.at[planes[slot], pl.ds(start, rows), :], 0, start)
+        send(lambda slot: u.at[0, slot, pl.ds(PAD + start, rows), :], 0, start)
     for load in loads[4:]:
         load.start()
 
@@ -170,7 +171,7 @@
                     use(slot, row, columns(t), value, lap)
                 above, here, here_down = here_up, below, below_down
 
-    for load in loads[:4]:
+    for load in loads[2:4]:
         load.wait()
 
     def greet(at):
@@ -229,18 +230,15 @@
 
     lax.fori_loop(0, CHUNKS, turn, 0)
 
-    def tile_copy(source, target, stage, slot, device):
+    def pair_copy(stage, device, slot=0):
         return pltpu.make_async_remote_copy(
-            src_ref=source,
-            dst_ref=target,
+            src_ref=totals.at[stage],
+            dst_ref=inbox.at[stage],
             send_sem=tot_send.at[stage, slot],
             recv_sem=tot_recv.at[stage, slot],
             device_id=(device,),
             device_id_type=MESH,
         )
-
-    def pair_copy(stage, device, slot=0):
-        return tile_copy(totals.at[stage], inbox.at[stage], stage, slot, device)
 
     def pair_sends(stage, act):
         if stage == 0:
@@ -251,7 +249,7 @@
                 @pl.when(jnp.logical_and(core == sender, upper == (step == -1)))
                 def _():
                     for c in range(2):
-                        act(tile_copy(totals.at[stage], inbox.at[stage], stage, c, chip_x(step) + c))
+                        act(pair_copy(stage, chip_x(step) + c, c))
         else:
             upper = lax.rem(row + stage - 3, 2) == 1
             act(pair_copy(stage, jnp.where(upper, chip_y(-1), chip_y(1))))
@@ -259,20 +257,26 @@
     def pair_there(stage):
         return stage == 0 or (x, x // 2, y, y // 2)[stage - 1] > 1
 
-    def layer_copies(act):
-        for step in range(1, z):
-            device = lax.rem(depth + step, z) * layer + lax.rem(me, layer)
-            act(step, device)
+    def layer_copies():
+        return [
+            pltpu.make_async_remote_copy(
+                src_ref=layers.at[depth],
+                dst_ref=layers.at[depth],
+                send_sem=layer_send.at[step],
+                recv_sem=layer_recv.at[step],
+                device_id=(lax.rem(depth + step, z) * layer + lax.rem(me, layer),),
+                device_id_type=MESH,
+            )
+            for step in range(1, z)
+        ]
 
     def exchange(stage):
         if stage < PAIRS:
             if pair_there(stage):
                 pair_sends(stage, lambda copy: copy.start())
         else:
-            def start(step, device):
-                tile_copy(layers.at[depth], layers.at[depth], stage, step, device).start()
-
-            layer_copies(start)
+            for copy in layer_copies():
+                copy.start()
 
     def collect(stage):
         if stage < PAIRS:
@@ -289,10 +293,8 @@
                 pair_copy(stage, beside).wait_recv()
             totals[stage + 1] = totals[stage] + inbox[stage]
         else:
-            def finish(step, device):
-                tile_copy(layers.at[depth], layers.at[depth], stage, step, device).wait()
-
-            layer_copies(finish)
+            for copy in layer_copies():
+                copy.wait()
             total = layers[0]
             for slot in range(1, z):
                 total = total + layers[slot]
@@ -330,25 +332,41 @@
 
     lax.fori_loop(0, (ITERS - 1) * CHUNKS, adjoint, 0)
 
-    def finish(chunk, carry):
+    def finish(factor, chunk, carry):
         start = pl.multiple_of(chunk * rows, rows)
         arrived(2 * ITERS - 1, start)
 
         def use(slot, row, cols, value, lap):
             at = (slot, pl.ds(row, SUB), cols)
-            lam[at] = lam[at] + time_step * lap
+            fresh = lam[at] + time_step * lap
+            lam[at] = fresh if factor is None else fresh * factor
 
         laplace(mu, ITERS - 1, 2 * ITERS - 1, start, use)
         return carry
 
-    lax.fori_loop(0, CHUNKS, finish, 0)
+    lax.fori_loop(0, SUM_CHUNK, functools.partial(finish, None), 0)
+
     collect(PAIRS)
-    tot_out[...] = totals[PAIRS + 1]
+    total = jnp.sum(totals[PAIRS + 1], axis=0, keepdims=True)
+    total = jnp.sum(total, axis=1, keepdims=True)
+    misfit = jnp.sqrt(jnp.broadcast_to(total, (SUB, LANE)) / (n * 2 * ny * nx) + 1e-06)
+    factor = 1.0 / misfit
+    misfit_out[...] = misfit
+
+    def divide(field, block, carry):
+        row = pl.ds(pl.multiple_of(block * SUB, SUB), SUB)
+        for slot in range(2):
+            for t in range(tiles):
+                at = (slot, row, columns(t))
+                field[at] = field[at] * factor
+        return carry
+
+    lax.fori_loop(0, ny // SUB, functools.partial(divide, grad), 0)
+    lax.fori_loop(0, SUM_CHUNK * rows // SUB, functools.partial(divide, lam), 0)
+    lax.fori_loop(SUM_CHUNK, CHUNKS, functools.partial(finish, factor), 0)
 
     for step in range(2 * ITERS):
         def whole(slot):
-            if step == 0:
-                return u_hbm.at[planes[slot]]
             return (u.at[step, slot] if step < ITERS else mu.at[step - ITERS, slot]).at[pl.ds(PAD, ny), :]
 
         @pl.when(inner)
@@ -358,25 +376,15 @@
         copy_out(whole(1), step, 1, 0, ny, beside).wait_send()
 
 
-def scale_kernel(cells, grad, lam, tile, grad_out, lam_out, misfit_out, scaled_grad, scaled_lam, out_sem):
+def write_kernel(grad, lam, misfit, grad_out, lam_out, misfit_out, out_sem):
     core = lax.rem(lax.axis_index("gz"), 2)
-    ny = grad.shape[1]
-    rows = ny // PIECES
-    misfit = jnp.sqrt(jnp.sum(tile[...], keepdims=True) / cells + 1e-06)
-    factor = 1.0 / misfit
-    copies = []
-    for which, (source, scaled, target) in enumerate(((grad, scaled_grad, grad_out), (lam, scaled_lam, lam_out))):
-        for slot in range(2):
-            for piece in range(PIECES):
-                part = pl.ds(piece * rows, rows)
-                scaled[slot, part, :] = source[slot, part, :] * factor
-                plane = core if slot == 0 else 1 - core
-                copies.append(
-                    pltpu.make_async_copy(
-                        scaled.at[slot, part, :], target.at[plane, part, :], out_sem.at[which, slot, piece]
-                    )
-                )
-                copies[-1].start()
+    copies = [
+        pltpu.make_async_copy(source.at[slot], target.at[core if slot == 0 else 1 - core], out_sem.at[which, slot])
+        for which, (source, target) in enumerate(((grad, grad_out), (lam, lam_out)))
+        for slot in range(2)
+    ]
+    for copy in copies:
+        copy.start()
     misfit_out[0, 0] = misfit[0, 0]
     for copy in copies:
         copy.wait()
@@ -389,7 +397,7 @@
     near = pl.BlockSpec(memory_space=pltpu.VMEM)
     slab = jax.ShapeDtypeStruct(coefficient.shape, jnp.float32)
     padded = (ITERS, depth, ny + 2 * PAD, nx)
-    gradient, adjoint, tile = pl.pallas_call(
+    gradient, adjoint, misfit = pl.pallas_call(
         functools.partial(kernel, n, ny, nx),
         out_shape=(slab, slab, jax.ShapeDtypeStruct((SUB, LANE), jnp.float32)),
         in_specs=[far] * 4,
@@ -407,9 +415,11 @@
             pltpu.VMEM((layers, SUB, LANE), jnp.float32),
             pltpu.SemaphoreType.DMA((4, 2)),
             pltpu.SemaphoreType.DMA((2 * ITERS, 2)),
-            pltpu.SemaphoreType.DMA((2 * ITERS, 2, CHUNKS)),
-            pltpu.SemaphoreType.DMA((PAIRS + 1, max(layers, 2))),
-            pltpu.SemaphoreType.DMA((PAIRS + 1, max(layers, 2))),
+            pltpu.SemaphoreType.DMA((2, 2, CHUNKS)),
+            pltpu.SemaphoreType.DMA((PAIRS, 2)),
+            pltpu.SemaphoreType.DMA((PAIRS, 2)),
+            pltpu.SemaphoreType.DMA((layers,)),
+            pltpu.SemaphoreType.DMA((layers,)),
             pltpu.SemaphoreType.REGULAR((3,)),
         ],
         compiler_params=pltpu.CompilerParams(
@@ -417,17 +427,15 @@
         ),
     )(coefficient, initial_field, observed, misfit_weight)
     gradient, adjoint, misfit = pl.pallas_call(
-        functools.partial(scale_kernel, n * depth * ny * nx),
+        write_kernel,
         out_shape=(slab, slab, jax.ShapeDtypeStruct((1, 1), jnp.float32)),
         in_specs=[near] * 3,
         out_specs=(far, far, pl.BlockSpec(memory_space=pltpu.SMEM)),
         scratch_shapes=[
-            pltpu.VMEM((depth, ny, nx), jnp.float32),
-            pltpu.VMEM((depth, ny, nx), jnp.float32),
-            pltpu.SemaphoreType.DMA((2, 2, PIECES)),
+            pltpu.SemaphoreType.DMA((2, 2)),
         ],
-        compiler_params=pltpu.CompilerParams(vmem_limit_bytes=8 * 1024 * 1024),
-    )(gradient, adjoint, tile)
+        compiler_params=pltpu.CompilerParams(vmem_limit_bytes=4 * 1024 * 1024),
+    )(gradient, adjoint, misfit)
     return gradient, adjoint, misfit.reshape(())
 
 

time: 105 us -> 103 us (0.981)
  Pallas kernels: 105 us -> 103 us
    pallas_call x1, Pallas kernels: 102 us -> 100 us  [on_device(): pl.pallas_call(functools.partial(kernel, n, ny, nx), out_shape=(slab, sla...]
where the time goes in v5:
time: 103 us
  Pallas kernels  103 us (100%)
    pallas_call x1, Pallas kernels, on_device(): pl.pallas_call(functools.partial(kernel, n, ny, nx), out_shape=(slab, sla...  100 us
    pallas_call x1, Pallas kernels, on_device(): pl.pallas_call(write_kernel, out_shape=(slab, slab, jax.ShapeDtypeStruct(...  2.57 us

profile of v5, /device:TPU:127, one launch (start us, length us, event | category | flops | bytes accessed | tf_op | source)
XLA Modules:
  0.0 103.4 jit_solution(12951395169425399124)
XLA Ops:
  0.6 100.2 %shard_map.67 = (f32[2,512,512]{2,1,0:T(8,128)S(1)}, f32[2,512,512]{2,1,0:T(8,128)S(1)}, f32[8,128]{1,0:T(8,128)S(1)}) custom-call(f32[2,512,512]{2,1,0:T(8,128)} %c_hbm.1, f32[2,512,512]{2,1,0:T(8,128)} %u_hbm.1, f32[2,512,512]{2,1,0:T(8,128)} %o_hbm.1, f32[2,512,512]{2,1,0:T(8,128)} %w_hbm.1), custom_call_target="tpu_custom_call" | custom-call | tf_op jit(solution)/shard_map/pallas_call | solution.py:400
  100.8 2.6 %shard_map.68 = (f32[2,512,512]{2,1,0:T(8,128)}, f32[2,512,512]{2,1,0:T(8,128)}, f32[1,1]{1,0:T(1,128)}) custom-call(f32[2,512,512]{2,1,0:T(8,128)S(1)} %get-tuple-element.9.grad, f32[2,512,512]{2,1,0:T(8,128)S(1)} %get-tuple-element.10.lam, f32[8,128]{1,0:T(8,128)S(1)} %get-tuple-element.11.misfit), custom_call_target="tpu_custom_call" | custom-call | tf_op jit(solution)/shard_map/pallas_call | solution.py:429

commit v6 on v5

--- a/solution.py
+++ b/solution.py
@@ -25,12 +25,16 @@
     return x, y, n // (2 * x * y)
 
 
+def wait_for(ref, semaphore):
+    pltpu.make_async_copy(ref, ref, semaphore).wait()
+
+
 def kernel(
     n, ny, nx,
     c_hbm, u_hbm, o_hbm, w_hbm,
     grad, lam, misfit_out,
     u, mu, slopes, c, o, w, ghost, totals, inbox, layers,
-    load_sem, send_sem, recv_sem, tot_send, tot_recv, layer_send, layer_recv, hello,
+    load_sem, send_sem, recv_sem, tot_send, tot_recv, layer_sem, hello,
 ):
     me = lax.axis_index("gz")
     core = lax.rem(me, 2)
@@ -70,7 +74,7 @@
     for index, (source, target) in enumerate(((u_hbm, u), (c_hbm, c), (o_hbm, o), (w_hbm, w))):
         for slot in range(2):
             place = u.at[0, slot, pl.ds(PAD, ny), :] if target is u else target.at[slot]
-            loads.append(pltpu.make_async_copy(source.at[planes[slot]], place, load_sem.at[index, slot]))
+            loads.append(pltpu.make_async_copy(source.at[planes[slot]], place, load_sem.at[index]))
     barrier = pltpu.get_barrier_semaphore()
 
     def ready(device):
@@ -85,16 +89,15 @@
     others = along_z(1, ready) if reach else 0
     for load in loads[:4]:
         load.start()
-    for load in loads[:2]:
-        load.wait()
+    wait_for(u.at[0, :, pl.ds(PAD, ny), :], load_sem.at[0])
     pl.semaphore_wait(barrier, len(partners) + line_end.astype(jnp.int32) + others)
 
     def copy_out(source, step, slot, start, count, target):
         return pltpu.make_async_remote_copy(
             src_ref=source,
             dst_ref=ghost.at[step, slot, pl.ds(start, count), :],
-            send_sem=send_sem.at[step, slot],
-            recv_sem=recv_sem.at[step % 2 if isinstance(step, int) else lax.rem(step, 2), slot, start // rows],
+            send_sem=send_sem.at[slot],
+            recv_sem=recv_sem.at[lax.rem(step, 2), start // rows],
             device_id=(target,),
             device_id_type=MESH,
         )
@@ -109,9 +112,13 @@
     def arrived(step, start):
         @pl.when(inner)
         def _():
-            copy_out(ghost.at[step, 0, pl.ds(start, rows), :], step, 0, start, rows, beyond).wait_recv()
-
-        copy_out(ghost.at[step, 1, pl.ds(start, rows), :], step, 1, start, rows, beside).wait_recv()
+            both = ghost.at[step, :, pl.ds(start, rows), :]
+            wait_for(both, recv_sem.at[lax.rem(step, 2), start // rows])
+
+        @pl.when(jnp.logical_not(inner))
+        def _():
+            one = ghost.at[step, 1, pl.ds(start, rows), :]
+            wait_for(one, recv_sem.at[lax.rem(step, 2), start // rows])
 
     for chunk in range(CHUNKS):
         start = chunk * rows
@@ -171,8 +178,7 @@
                     use(slot, row, columns(t), value, lap)
                 above, here, here_down = here_up, below, below_down
 
-    for load in loads[2:4]:
-        load.wait()
+    wait_for(c, load_sem.at[1])
 
     def greet(at):
         for turn in range(len(reach) + 1):
@@ -203,8 +209,8 @@
         return carry
 
     lax.fori_loop(0, (ITERS - 1) * CHUNKS, forward, 0)
-    for load in loads[4:]:
-        load.wait()
+    wait_for(o, load_sem.at[2])
+    wait_for(w, load_sem.at[3])
     totals[0] = nothing
 
     def turn(chunk, carry):
@@ -234,8 +240,8 @@
         return pltpu.make_async_remote_copy(
             src_ref=totals.at[stage],
             dst_ref=inbox.at[stage],
-            send_sem=tot_send.at[stage, slot],
-            recv_sem=tot_recv.at[stage, slot],
+            send_sem=tot_send.at[slot],
+            recv_sem=tot_recv.at[stage],
             device_id=(device,),
             device_id_type=MESH,
         )
@@ -262,8 +268,8 @@
             pltpu.make_async_remote_copy(
                 src_ref=layers.at[depth],
                 dst_ref=layers.at[depth],
-                send_sem=layer_send.at[step],
-                recv_sem=layer_recv.at[step],
+                send_sem=layer_sem.at[0],
+                recv_sem=layer_sem.at[1],
                 device_id=(lax.rem(depth + step, z) * layer + lax.rem(me, layer),),
                 device_id_type=MESH,
             )
@@ -284,17 +290,12 @@
                 totals[stage + 1] = totals[stage]
                 return
             pair_sends(stage, lambda copy: copy.wait_send())
-            if 0 < stage < 3:
-                for c in range(2):
-                    @pl.when(core == c)
-                    def _():
-                        pair_copy(stage, beside, c).wait_recv()
-            else:
-                pair_copy(stage, beside).wait_recv()
+            pair_copy(stage, beside).wait_recv()
             totals[stage + 1] = totals[stage] + inbox[stage]
         else:
-            for copy in layer_copies():
-                copy.wait()
+            if z > 1:
+                for index in range(2):
+                    wait_for(layers.at[pl.ds(0, z - 1)], layer_sem.at[index])
             total = layers[0]
             for slot in range(1, z):
                 total = total + layers[slot]
@@ -365,15 +366,11 @@
     lax.fori_loop(0, SUM_CHUNK * rows // SUB, functools.partial(divide, lam), 0)
     lax.fori_loop(SUM_CHUNK, CHUNKS, functools.partial(finish, factor), 0)
 
-    for step in range(2 * ITERS):
-        def whole(slot):
-            return (u.at[step, slot] if step < ITERS else mu.at[step - ITERS, slot]).at[pl.ds(PAD, ny), :]
-
-        @pl.when(inner)
-        def _():
-            copy_out(whole(0), step, 0, 0, ny, beyond).wait_send()
-
-        copy_out(whole(1), step, 1, 0, ny, beside).wait_send()
+    @pl.when(inner)
+    def _():
+        wait_for(ghost.at[:, 0], send_sem.at[0])
+
+    wait_for(ghost.at[:, 1], send_sem.at[1])
 
 
 def write_kernel(grad, lam, misfit, grad_out, lam_out, misfit_out, out_sem):
@@ -413,13 +410,12 @@
             pltpu.VMEM((PAIRS + 2, SUB, LANE), jnp.float32),
             pltpu.VMEM((PAIRS, SUB, LANE), jnp.float32),
             pltpu.VMEM((layers, SUB, LANE), jnp.float32),
-            pltpu.SemaphoreType.DMA((4, 2)),
-            pltpu.SemaphoreType.DMA((2 * ITERS, 2)),
-            pltpu.SemaphoreType.DMA((2, 2, CHUNKS)),
-            pltpu.SemaphoreType.DMA((PAIRS, 2)),
-            pltpu.SemaphoreType.DMA((PAIRS, 2)),
-            pltpu.SemaphoreType.DMA((layers,)),
-            pltpu.SemaphoreType.DMA((layers,)),
+            pltpu.SemaphoreType.DMA((4,)),
+            pltpu.SemaphoreType.DMA((2,)),
+            pltpu.SemaphoreType.DMA((2, CHUNKS)),
+            pltpu.SemaphoreType.DMA((2,)),
+            pltpu.SemaphoreType.DMA((PAIRS,)),
+            pltpu.SemaphoreType.DMA((2,)),
             pltpu.SemaphoreType.REGULAR((3,)),
         ],
         compiler_params=pltpu.CompilerParams(

time: 103 us -> 103 us (level)
  no operation moved by 1% of the time
where the time goes in v6:
time: 103 us
  Pallas kernels  102 us (99%)
    pallas_call x1, Pallas kernels, on_device(): pl.pallas_call(functools.partial(kernel, n, ny, nx), out_shape=(slab, sla...  99.6 us
    pallas_call x1, Pallas kernels, on_device(): pl.pallas_call(write_kernel, out_shape=(slab, slab, jax.ShapeDtypeStruct(...  2.57 us

profile of v6, /device:TPU:127, one launch (start us, length us, event | category | flops | bytes accessed | tf_op | source)
XLA Modules:
  0.0 102.8 jit_solution(12619268008089960675)
XLA Ops:
  0.6 99.6 %shard_map.67 = (f32[2,512,512]{2,1,0:T(8,128)S(1)}, f32[2,512,512]{2,1,0:T(8,128)S(1)}, f32[8,128]{1,0:T(8,128)S(1)}) custom-call(f32[2,512,512]{2,1,0:T(8,128)} %c_hbm.1, f32[2,512,512]{2,1,0:T(8,128)} %u_hbm.1, f32[2,512,512]{2,1,0:T(8,128)} %o_hbm.1, f32[2,512,512]{2,1,0:T(8,128)} %w_hbm.1), custom_call_target="tpu_custom_call" | custom-call | tf_op jit(solution)/shard_map/pallas_call | solution.py:397
  100.3 2.6 %shard_map.68 = (f32[2,512,512]{2,1,0:T(8,128)}, f32[2,512,512]{2,1,0:T(8,128)}, f32[1,1]{1,0:T(1,128)}) custom-call(f32[2,512,512]{2,1,0:T(8,128)S(1)} %get-tuple-element.9.grad, f32[2,512,512]{2,1,0:T(8,128)S(1)} %get-tuple-element.10.lam, f32[8,128]{1,0:T(8,128)S(1)} %get-tuple-element.11.misfit), custom_call_target="tpu_custom_call" | custom-call | tf_op jit(solution)/shard_map/pallas_call | solution.py:425

commit v7 on v6

--- a/solution.py
+++ b/solution.py
@@ -373,7 +373,7 @@
     wait_for(ghost.at[:, 1], send_sem.at[1])
 
 
-def write_kernel(grad, lam, misfit, grad_out, lam_out, misfit_out, out_sem):
+def write_kernel(grad, lam, misfit, grad_out, lam_out, misfit_out, scalar, out_sem):
     core = lax.rem(lax.axis_index("gz"), 2)
     copies = [
         pltpu.make_async_copy(source.at[slot], target.at[core if slot == 0 else 1 - core], out_sem.at[which, slot])
@@ -382,7 +382,9 @@
     ]
     for copy in copies:
         copy.start()
-    misfit_out[0, 0] = misfit[0, 0]
+    scalar[0, 0] = misfit[0, 0]
+    copies.append(pltpu.make_async_copy(scalar, misfit_out, out_sem.at[2, 0]))
+    copies[-1].start()
     for copy in copies:
         copy.wait()
 
@@ -426,9 +428,10 @@
         write_kernel,
         out_shape=(slab, slab, jax.ShapeDtypeStruct((1, 1), jnp.float32)),
         in_specs=[near] * 3,
-        out_specs=(far, far, pl.BlockSpec(memory_space=pltpu.SMEM)),
+        out_specs=(far,) * 3,
         scratch_shapes=[
-            pltpu.SemaphoreType.DMA((2, 2)),
+            pltpu.SMEM((1, 1), jnp.float32),
+            pltpu.SemaphoreType.DMA((3, 2)),
         ],
         compiler_params=pltpu.CompilerParams(vmem_limit_bytes=4 * 1024 * 1024),
     )(gradient, adjoint, misfit)

time: 103 us -> 102 us (level)
  no operation moved by 1% of the time
where the time goes in v7:
time: 102 us
  Pallas kernels  102 us (100%)
    pallas_call x1, Pallas kernels, on_device(): pl.pallas_call(functools.partial(kernel, n, ny, nx), out_shape=(slab, sla...  99.6 us
    pallas_call x1, Pallas kernels, on_device(): pl.pallas_call(write_kernel, out_shape=(slab, slab, jax.ShapeDtypeStruct(...  2.08 us

profile of v7, /device:TPU:127, one launch (start us, length us, event | category | flops | bytes accessed | tf_op | source)
XLA Modules:
  0.0 102.3 jit_solution(2764578269303091680)
XLA Ops:
  0.6 99.6 %shard_map.67 = (f32[2,512,512]{2,1,0:T(8,128)S(1)}, f32[2,512,512]{2,1,0:T(8,128)S(1)}, f32[8,128]{1,0:T(8,128)S(1)}) custom-call(f32[2,512,512]{2,1,0:T(8,128)} %c_hbm.1, f32[2,512,512]{2,1,0:T(8,128)} %u_hbm.1, f32[2,512,512]{2,1,0:T(8,128)} %o_hbm.1, f32[2,512,512]{2,1,0:T(8,128)} %w_hbm.1), custom_call_target="tpu_custom_call" | custom-call | tf_op jit(solution)/shard_map/pallas_call | solution.py:399
  100.3 2.1 %shard_map.68 = (f32[2,512,512]{2,1,0:T(8,128)}, f32[2,512,512]{2,1,0:T(8,128)}, f32[1,1]{1,0:T(1,128)}) custom-call(f32[2,512,512]{2,1,0:T(8,128)S(1)} %get-tuple-element.9.grad, f32[2,512,512]{2,1,0:T(8,128)S(1)} %get-tuple-element.10.lam, f32[8,128]{1,0:T(8,128)S(1)} %get-tuple-element.11.misfit), custom_call_target="tpu_custom_call" | custom-call | tf_op jit(solution)/shard_map/pallas_call | solution.py:427

commit v8 on v7

--- a/solution.py
+++ b/solution.py
@@ -10,13 +10,13 @@
 MESH = pl.DeviceIdType.MESH
 time_step = 0.125
 ITERS = 4
-CHUNKS = 8
+CHUNKS = 16
 PAD = 8
 SUB, LANE = 8, 128
-SUM_CHUNK = 5
+SUM_CHUNK = 11
 PAIRS = 5
-STAGE_TIMES = ((0, 2), (3, 6), (7, 10), (11, 14), (15, 18), (19, None))
-HELLO_TIMES = (2, 8, 14, 20)
+STAGE_TIMES = ((0, 4), (5, 12), (13, 20), (21, 28), (29, 36), (37, None))
+HELLO_TIMES = (4, 16, 28, 40)
 
 
 def torus(n):

time: 102 us -> 102 us (level)
  no operation moved by 1% of the time
where the time goes in v8:
time: 102 us
  Pallas kernels  102 us (100%)
    pallas_call x1, Pallas kernels, on_device(): pl.pallas_call(functools.partial(kernel, n, ny, nx), out_shape=(slab, sla...  99.7 us
    pallas_call x1, Pallas kernels, on_device(): pl.pallas_call(write_kernel, out_shape=(slab, slab, jax.ShapeDtypeStruct(...  2.08 us

profile of v8, /device:TPU:127, one launch (start us, length us, event | category | flops | bytes accessed | tf_op | source)
XLA Modules:
  0.0 102.4 jit_solution(4056126308852176756)
XLA Ops:
  0.6 99.7 %shard_map.67 = (f32[2,512,512]{2,1,0:T(8,128)S(1)}, f32[2,512,512]{2,1,0:T(8,128)S(1)}, f32[8,128]{1,0:T(8,128)S(1)}) custom-call(f32[2,512,512]{2,1,0:T(8,128)} %c_hbm.1, f32[2,512,512]{2,1,0:T(8,128)} %u_hbm.1, f32[2,512,512]{2,1,0:T(8,128)} %o_hbm.1, f32[2,512,512]{2,1,0:T(8,128)} %w_hbm.1), custom_call_target="tpu_custom_call" | custom-call | tf_op jit(solution)/shard_map/pallas_call | solution.py:399
  100.3 2.1 %shard_map.68 = (f32[2,512,512]{2,1,0:T(8,128)}, f32[2,512,512]{2,1,0:T(8,128)}, f32[1,1]{1,0:T(1,128)}) custom-call(f32[2,512,512]{2,1,0:T(8,128)S(1)} %get-tuple-element.9.grad, f32[2,512,512]{2,1,0:T(8,128)S(1)} %get-tuple-element.10.lam, f32[8,128]{1,0:T(8,128)S(1)} %get-tuple-element.11.misfit), custom_call_target="tpu_custom_call" | custom-call | tf_op jit(solution)/shard_map/pallas_call | solution.py:427
